TPU v7x, 32 devices: a whole 2x2x4 slice. The times are simulated.
32 devices in a mesh: site: 4 (over z), py: 2 (over x), px: 2 (over y), pz: 2 (over core).
Axes of the slice: x: 2, y: 2, z: 4, core: 2. Of those that a mesh axis runs over, the one named last changes fastest.
Arguments:
- initial_heat_state: float32 [32, 128, 64, 128], P(('site', 'py'), 'px', 'pz'), parts along dimension 0, may hold values from 0.2 to 1.8
- scaled_speed_north: float32 [32, 128, 64, 128], P(('site', 'py'), 'px', 'pz'), parts along dimension 0, may hold values from -0.3 to 0.3
- scaled_speed_east: float32 [32, 128, 64, 128], P(('site', 'py'), 'px', 'pz'), parts along dimension 0, may hold values from -0.3 to 0.3
- scaled_speed_upward: float32 [32, 128, 64, 128], P(('site', 'py'), 'px', 'pz'), parts along dimension 0, may hold values from -0.3 to 0.3
Outputs:
- temperature_end: float32 [32, 128, 64, 128], P(('site', 'py'), 'px', 'pz'), parts along dimension 0
There are 4 independent parts, one for each index of `site`. A program takes and returns all parts, laid end to end along the dimension named above; each array names one. Nothing has to cross between parts.
All inputs are finite; a program needn't handle non-finite values.
Results may differ from a plain program's by a relative error of at most 0.00002.
Values sent between devices are 32-bit elements; how exact they have to be, the bound alone decides.
No kernel may reach another device: no remote copies, remote signals or barrier semaphores. Data moves between devices by JAX's collectives and lax.ppermute only.
A program may use at most 256 MiB of HBM per device.

v0:
```python
import functools

import jax
import jax.numpy as jnp
from jax import lax
from jax.experimental import pallas as pl
from jax.experimental.pallas import tpu as pltpu
from jax.sharding import PartitionSpec as P


STEPS = 4
RATE = 0.05
CHUNKS = 2
ROWS = 8
FIRST = 16
VMEM = pltpu.VMEM


def cuts(extent):
    pieces = CHUNKS if extent % (ROWS * CHUNKS) == 0 else 1
    width = extent // pieces
    return [(start, width) for start in range(0, extent, width)]


def split(start, width, first):
    if 0 < first < width:
        return [(start, first), (start + first, width - first)]
    return [(start, width)]


def exchange(faces, axis):
    count = lax.axis_size(axis)
    if count == 1:
        return []
    if count == 2:
        return [lax.ppermute(faces[0], axis, [(0, 1), (1, 0)])]
    low, high = faces
    return [
        lax.ppermute(high, axis, [(i, i + 1) for i in range(count - 1)]),
        lax.ppermute(low, axis, [(i + 1, i) for i in range(count - 1)]),
    ]


def face_count(axis):
    return min(lax.axis_size(axis) - 1, 2)


def on_sides(axis, low, high):
    count = lax.axis_size(axis)
    if count == 1:
        return
    place = lax.axis_index(axis)
    pl.when(place > 0)(low)
    pl.when(place < count - 1)(high)


def send_sides(axis, faces, low, high):
    if len(faces) == 1:
        on_sides(axis, lambda: low(faces[0]), lambda: high(faces[0]))
    elif faces:
        low(faces[0])
        high(faces[1])


def flat(ref):
    rows = 1
    for extent in ref.shape[:-1]:
        rows *= extent
    return ref.reshape(rows, ref.shape[-1])


def copy_column_layer(parts, layer, face):
    for part, start in parts:
        ny, nx, nz, _ = part.shape
        rows = flat(part)
        for y in range(ny):
            for x in range(0, nx, ROWS):
                face[y, pl.ds(start + x, ROWS), :] = rows[pl.ds((y * nx + x) * nz + layer, ROWS, stride=nz), :]


def send_x_and_z(parts, x_faces, z_faces):
    first, last = parts[0][0], parts[-1][0]

    def x_layer(part, row):
        def write(face):
            face[...] = part[:, row]

        return write

    send_sides("px", x_faces, x_layer(first, 0), x_layer(last, last.shape[1] - 1))
    nz = first.shape[2]
    send_sides(
        "pz",
        z_faces,
        lambda face: copy_column_layer(parts, 0, face),
        lambda face: copy_column_layer(parts, nz - 1, face),
    )


def load(sources, places, sem, slot, priority=0):
    copies = [
        pltpu.make_async_copy(source, place, sem.at[slot + i]) for i, (source, place) in enumerate(zip(sources, places))
    ]
    for copy in copies:
        copy.start(priority=priority)
    for copy in copies:
        copy.wait()


def first_y_kernel(pieces, sides, field, after, *rest):
    *rest, sem = rest
    speeds, rest = (rest[:3], rest[3:]) if len(rest) > len(pieces) * sides else ([], rest)
    faces, held = rest[: len(pieces) * sides], rest[len(pieces) * sides :]
    if speeds:
        pl.when(lax.axis_index("pz") % 2 == 1)(lambda: load(speeds, held, sem, len(faces)))
    top = field.shape[0] - 1

    def fetch(layers):
        sources = [field.at[layer, pl.ds(start, width)] for start, width in pieces for layer in layers]
        load(sources, faces, sem, 0, 1 - len(speeds) // 3)

    if sides == 1:
        fetch([top * (1 - lax.axis_index("py"))])
    else:
        fetch([0, top])


def load_field_kernel(nx_faces, field, after, copy_of, *rest):
    faces, sem = rest[:-1], rest[-1]
    copy = pltpu.make_async_copy(field, copy_of, sem)
    copy.start()
    copy.wait()
    send_x_and_z([(copy_of, 0)], faces[:nx_faces], faces[nx_faces:])


def load_speeds_kernel(partly, north, east, upward, after, *rest):
    *held, sem = rest[3 * partly :]
    fetch = lambda: load((north, east, upward), held, sem, 0)
    if partly:
        pl.when(lax.axis_index("pz") % 2 == 0)(fetch)
    else:
        fetch()


def march(out, start, width, extent, parts, speeds, x_halo, z_halo):
    north, east, upward = speeds
    ny, _, nz, lanes = out.shape
    layer_of = lax.broadcasted_iota(jnp.int32, (nz, lanes), 0)

    def find(x):
        for part, origin in reversed(parts):
            if x >= origin:
                return part, x - origin

    centre_part, centre_base = find(start)

    def row(x_local, left, right):
        centre = [centre_part[y, centre_base + x_local] for y in range(ny)]
        for y in range(ny):
            here = centre[y]
            above = centre[y + 1] if y + 1 < ny else None
            below = centre[y - 1] if y > 0 else None
            up = jnp.where(layer_of == nz - 1, 0.0, pltpu.roll(here, nz - 1, 0))
            down = jnp.where(layer_of == 0, 0.0, pltpu.roll(here, 1, 0))
            total = here * (1.0 - 6.0 * RATE)
            spread = up + down
            total -= upward[y, start + x_local] * (up - down)
            for speed, higher, lower in ((north, above, below), (east, right and right(y), left and left(y))):
                if higher is None and lower is None:
                    continue
                rate = speed[y, start + x_local]
                if lower is None:
                    total -= rate * higher
                    spread += higher
                elif higher is None:
                    total += rate * lower
                    spread += lower
                else:
                    total -= rate * (higher - lower)
                    spread += higher + lower
            out[y, x_local] = total + RATE * spread

    def at(part, index):
        return lambda y: part[y, index]

    def edge(x):
        return at(*find(x)) if 0 <= x < extent else None

    row(0, edge(start - 1), edge(start + 1))

    @pl.loop(1, width - 1)
    def _(x):
        row(x, at(centre_part, centre_base + x - 1), at(centre_part, centre_base + x + 1))

    row(width - 1, edge(start + width - 2), edge(start + width))

    def x_side(x, sign, halo):
        def add():
            for y in range(ny):
                out[y, x - start] += (RATE + sign * east[y, x]) * halo[y]

        return add

    if x_halo:
        nothing = lambda: None
        on_sides(
            "px",
            x_side(0, 1.0, x_halo[0]) if start == 0 else nothing,
            x_side(extent - 1, -1.0, x_halo[-1]) if start + width == extent else nothing,
        )

    def z_side(layer, sign, halo):
        def add():
            out_rows, up_rows = flat(out), flat(upward)
            for y in range(ny):
                for x in range(0, width, ROWS):
                    mine = pl.ds((y * width + x) * nz + layer, ROWS, stride=nz)
                    speed = up_rows[pl.ds((y * extent + start + x) * nz + layer, ROWS, stride=nz), :]
                    out_rows[mine, :] = out_rows[mine, :] + (RATE + sign * speed) * halo[y, pl.ds(start + x, ROWS), :]

        return add

    if z_halo:
        on_sides("pz", z_side(0, 1.0, z_halo[0]), z_side(nz - 1, -1.0, z_halo[-1]))


def taker(refs):
    refs = list(refs)

    def take(count):
        taken, refs[:] = refs[:count], refs[count:]
        return taken

    return take


def step_kernel(plan, *refs):
    take = taker(refs)
    start, width, extent, sides = plan["start"], plan["width"], plan["extent"], plan["sides"]
    parts = list(zip(take(len(plan["starts"])), plan["starts"]))
    speeds = take(3)
    x_halo, z_halo = take(sides[1]), take(sides[2])
    y_halos = [(piece, take(sides[0])) for piece in plan["arrive"]]
    earlier = list(zip(take(len(plan["earlier"])), plan["earlier"]))
    (out,) = take(1)
    y_faces = [(piece, take(sides[0])) for piece in plan["leave"]]
    north, ny = speeds[0], out.shape[0]

    march(out, start, width, extent, parts, speeds, x_halo, z_halo)

    def y_side(layer, sign, side):
        def add():
            for (begin, count), halo in y_halos:

                @pl.loop(0, count)
                def _(x):
                    out[layer, begin - start + x] += (RATE + sign * north[layer, begin + x]) * halo[side][x]

        return add

    if sides[0]:
        on_sides("py", y_side(0, 1.0, 0), y_side(ny - 1, -1.0, sides[0] - 1))

    def y_layer(layer, begin, count):
        def write(face):
            face[...] = out[layer, pl.ds(begin - start, count)]

        return write

    for (begin, count), faces in y_faces:
        send_sides("py", faces, y_layer(0, begin, count), y_layer(ny - 1, begin, count))
    if start + width == extent:
        x_faces, z_faces = take(sides[1]), take(sides[2])
        send_x_and_z(earlier + [(out, start)], x_faces, z_faces)


def last_inner_kernel(plan, *refs):
    take = taker(refs)
    extent, sides = plan["extent"], plan["sides"]
    parts = list(zip(take(len(plan["starts"])), plan["starts"]))
    speeds = take(3)
    x_halo, z_halo = take(sides[1]), take(sides[2])
    (whole,) = take(1)
    waiting = take(sides[0])
    outs = take(len(plan["chunks"]))
    (sem,) = take(1)
    ny = whole.shape[0]

    def ready(index, begin, count):
        start, width = plan["chunks"][index]
        return pltpu.make_async_copy(
            outs[index].at[pl.ds(begin, count)], whole.at[pl.ds(begin, count), pl.ds(start, width)], sem.at[index]
        )

    def put(index, start, width):
        def keep(layer):
            def write(face):
                face[pl.ds(start, width)] = outs[index][layer]

            return write

        send_sides("py", waiting, keep(0), keep(ny - 1))
        if sides[0] == 0:
            ready(index, 0, ny).start()
        elif sides[0] == 1:
            on_sides("py", ready(index, 1, ny - 1).start, ready(index, 0, ny - 1).start)
        elif ny > 2:
            ready(index, 1, ny - 2).start()

    for index, (start, width) in enumerate(plan["chunks"]):
        march(outs[index], start, width, extent, parts, speeds, x_halo, z_halo)
        put(index, start, width)
    for index in range(len(plan["chunks"])):
        count = ny - sides[0]
        if count > 0:
            ready(index, 0, count).wait()


def last_outer_kernel(piece, sides, north, *refs):
    take = taker(refs)
    waiting, halo = take(sides), take(sides)
    take(1)
    (whole,) = take(1)
    held = take(sides)
    (sem,) = take(1)
    begin, count = piece
    top = whole.shape[0] - 1

    def finish(layer, sign, side):
        def run():
            for x in range(count):
                rate = RATE + sign * north[layer, begin + x]
                held[side][x] = waiting[side][begin + x] + rate * halo[side][x]
            copy = pltpu.make_async_copy(held[side], whole.at[layer, pl.ds(begin, count)], sem.at[side])
            copy.start(priority=1)
            copy.wait()

        return run

    low, high = finish(0, 1.0, 0), finish(top, -1.0, sides - 1)
    if sides == 1:
        on_sides("py", low, high)
    else:
        low()
        high()


def body(field, north, east, upward):
    ny, nx, nz, lanes = field.shape
    sides = [face_count(axis) for axis in ("py", "px", "pz")]
    chunks = cuts(nx)
    in_vmem = pl.BlockSpec(memory_space=VMEM)
    anywhere = pl.BlockSpec(memory_space=pl.ANY)
    dma = pltpu.SemaphoreType.DMA
    params = pltpu.CompilerParams(vmem_limit_bytes=12 * 2**20)

    def vmem(*shape):
        return VMEM(shape, field.dtype)

    def call(kernel, outs, ins, in_specs=None, flops=0, **more):
        more.setdefault("out_specs", [in_vmem] * len(outs))
        return list(
            pl.pallas_call(
                kernel,
                out_shape=outs,
                in_specs=in_specs or [in_vmem] * len(ins),
                compiler_params=params,
                cost_estimate=pl.CostEstimate(flops=flops, bytes_accessed=0, transcendentals=0),
                **more,
            )(*ins)
        )

    def in_hbm(array):
        return pltpu.with_memory_space_constraint(array, pltpu.HBM)

    def send_y(pieces, faces):
        halos = []
        for i in range(len(pieces)):
            halos.append(exchange(faces[i * sides[0] : (i + 1) * sides[0]], "py"))
        return halos

    arrive = [split(*chunk, FIRST if index == 0 else 0) for index, chunk in enumerate(chunks)]
    pieces = [piece for chunk in arrive for piece in chunk]
    speeds = [in_hbm(speed) for speed in (north, east, upward)]
    halos, held, after = [], [], speeds[0]
    for group, early in ((pieces[:1], []), (pieces[1:], speeds)):
        if sides[0] == 0:
            halos += [[] for _ in group]
        elif group:
            shapes = [vmem(width, nz, lanes) for _, width in group for _ in range(sides[0])]
            made = call(
                functools.partial(first_y_kernel, group, sides[0]),
                shapes + [vmem(*field.shape)] * len(early),
                [in_hbm(field), after] + early,
                [anywhere] * (2 + len(early)),
                flops=10**6,
                scratch_shapes=[dma((len(shapes) + len(early),))],
            )
            faces, held = made[: len(shapes)], made[len(shapes) :]
            after = faces[0]
            halos += send_y(group, faces)
    x_shapes = [vmem(ny, nz, lanes)] * sides[1]
    z_shapes = [vmem(ny, nx, lanes)] * sides[2]
    field, *faces = call(
        functools.partial(load_field_kernel, sides[1]),
        [vmem(*field.shape)] + x_shapes + z_shapes,
        [in_hbm(field), after],
        [anywhere] * 2,
        flops=10**6,
        scratch_shapes=[dma],
    )
    x_halo, z_halo = exchange(faces[: sides[1]], "px"), exchange(faces[sides[1] :], "pz")
    speeds = call(
        functools.partial(load_speeds_kernel, len(held) > 0),
        [vmem(*field.shape)] * 3,
        speeds + [field] + held,
        [anywhere] * (4 + len(held)),
        flops=10**7,
        out_specs=[anywhere] * 3,
        input_output_aliases={4 + i: i for i in range(len(held))},
        scratch_shapes=[dma((3,))],
    )

    parts, starts = [field], [0]
    for step in range(STEPS - 1):
        new_parts, new_halos, new_arrive = [], [], []
        for index, chunk in enumerate(chunks):
            start, width = chunk
            last_chunk = index == len(chunks) - 1
            tail = step == STEPS - 2 and last_chunk
            leave = split(start, width, width - ROWS if tail else 0)
            plan = dict(
                start=start,
                width=width,
                extent=nx,
                starts=starts,
                sides=sides,
                arrive=arrive[index],
                leave=leave,
                earlier=[begin for begin, _ in chunks[:index]] if last_chunk else [],
            )
            mine, halos = halos[: len(arrive[index])], halos[len(arrive[index]) :]
            ins = parts + speeds + x_halo + z_halo + [half for piece in mine for half in piece]
            outs = [vmem(ny, width, nz, lanes)] + [vmem(count, nz, lanes) for _, count in leave for _ in range(sides[0])]
            if last_chunk:
                outs += x_shapes + z_shapes
                ins += new_parts
            made = call(functools.partial(step_kernel, plan), outs, ins, flops=20 * ny * width * nz * lanes)
            new_parts.append(made[0])
            faces, rest = made[1 : 1 + sides[0] * len(leave)], made[1 + sides[0] * len(leave) :]
            new_halos += send_y(leave, faces)
            new_arrive.append(leave)
        x_halo, z_halo = exchange(rest[: sides[1]], "px"), exchange(rest[sides[1] :], "pz")
        parts, starts, halos, arrive = new_parts, [begin for begin, _ in chunks], new_halos, new_arrive

    whole, *waiting = call(
        functools.partial(last_inner_kernel, dict(extent=nx, starts=starts, sides=sides, chunks=chunks)),
        [jax.ShapeDtypeStruct(parts[0].shape[:1] + (nx, nz, lanes), north.dtype)] + [vmem(nx, nz, lanes)] * sides[0],
        parts + speeds + x_halo + z_halo,
        flops=20 * ny * nx * nz * lanes,
        out_specs=[anywhere] + [in_vmem] * sides[0],
        scratch_shapes=[vmem(ny, width, nz, lanes) for _, width in chunks] + [dma((len(chunks),))],
    )
    if sides[0]:
        pieces = [piece for chunk in arrive for piece in chunk]
        for piece, halo in zip(pieces, halos):
            ins = speeds[:1] + waiting + halo + [whole]
            (whole,) = call(
                functools.partial(last_outer_kernel, piece, sides[0]),
                [jax.ShapeDtypeStruct(whole.shape, whole.dtype)],
                ins,
                [in_vmem] * (len(ins) - 1) + [anywhere],
                flops=3 * piece[1] * nz * lanes,
                out_specs=[anywhere],
                input_output_aliases={len(ins) - 1: 0},
                scratch_shapes=[vmem(piece[1], nz, lanes)] * sides[0] + [dma((sides[0],))],
            )
    return whole


def solution(mesh):
    spec = P(("site", "py"), "px", "pz", None)

    return jax.shard_map(body, mesh=mesh, in_specs=(spec,) * 4, out_specs=spec, check_vma=False)
```

profile of v0, /device:TPU:1, one launch (start us, length us, event | category | flops | bytes accessed | tf_op | source)
XLA Modules:
  0.0 98.8 jit_solution(16624913294322349131)
XLA Ops:
  1.0 5.8 %shard_map.47 = (f32[16,32,128]{2,1,0:T(8,128)S(1)}, f32[32,32,128]{2,1,0:T(8,128)S(1)}, f32[4,64,32,128]{3,2,1,0:T(8,128)S(1)}, f32[4,64,32,128]{3,2,1,0:T(8,128)S(1)}, f32[4,64,32,128]{3,2,1,0:T(8,128)S(1)}) custom-call(f32[4,64,32,128]{3,2,1,0:T(8,128)} %field.5, f32[16,32,128]{2,1,0:T(8,128)S(1)} %shard_map.46.after, f32[4,64,32,128]{3,2,1,0:T(8,128)} %north.1, ...), custom_call_target="tpu_custom_call" | custom-call | flops 1000000 | tf_op jit(solution)/shard_map/pallas_call | solution.py:363
  6.8 2.1 %collective-permute-start.4 = (f32[32,32,128]{2,1,0:T(8,128)S(1)}, f32[32,32,128]{2,1,0:T(8,128)S(1)}, u32[]{:S(2)}, u32[]{:S(2)}) collective-permute-start(f32[32,32,128]{2,1,0:T(8,128)S(1)} %get-tuple-element.48), channel_id=1, source_target_pairs={{0,4},{4,0},{1,5},{5,1},{2,6},{6,2},{3,7},{7,3},{8,12},{12,8},{9,1... | collective-permute-start | bytes 1572872 | tf_op jit(solution)/shard_map/ppermute | solution.py:36
  10.4 2.3 %shard_map.48 = (f32[4,64,32,128]{3,2,1,0:T(8,128)S(1)}, f32[4,32,128]{2,1,0:T(8,128)S(1)}, f32[4,64,128]{2,1,0:T(8,128)S(1)}) custom-call(f32[4,64,32,128]{3,2,1,0:T(8,128)} %field.5, f32[16,32,128]{2,1,0:T(8,128)S(1)} %get-tuple-element.37.after), custom_call_target="tpu_custom_call" | custom-call | flops 1000000 | tf_op jit(solution)/shard_map/pallas_call | solution.py:363
  14.1 2.1 %collective-permute-done.refs_4_ = f32[4,32,128]{2,1,0:T(8,128)S(1)} collective-permute-done((f32[4,32,128]{2,1,0:T(8,128)S(1)}, f32[4,32,128]{2,1,0:T(8,128)S(1)}, u32[]{:S(2)}, u32[]{:S(2)}) %collective-permute-start) | collective-permute-done | bytes 65568 | tf_op jit(solution)/shard_map/ppermute | solution.py:36
  16.3 9.5 %collective-permute-done.2.refs_6_ = f32[16,32,128]{2,1,0:T(8,128)S(1)} collective-permute-done((f32[16,32,128]{2,1,0:T(8,128)S(1)}, f32[16,32,128]{2,1,0:T(8,128)S(1)}, u32[]{:S(2)}, u32[]{:S(2)}) %collective-permute-start.2) | collective-permute-done | bytes 262176 | tf_op jit(solution)/shard_map/ppermute | solution.py:36
  25.7 2.8 %collective-permute-done.3.refs_7_ = f32[16,32,128]{2,1,0:T(8,128)S(1)} collective-permute-done((f32[16,32,128]{2,1,0:T(8,128)S(1)}, f32[16,32,128]{2,1,0:T(8,128)S(1)}, u32[]{:S(2)}, u32[]{:S(2)}) %collective-permute-start.3) | collective-permute-done | bytes 262176 | tf_op jit(solution)/shard_map/ppermute | solution.py:36
  28.5 2.0 %shard_map.50 = (f32[4,32,32,128]{3,2,1,0:T(8,128)S(1)}, f32[32,32,128]{2,1,0:T(8,128)S(1)}) custom-call(f32[4,64,32,128]{3,2,1,0:T(8,128)S(1)} %get-tuple-element.38.after.refs_0_, f32[4,64,32,128]{3,2,1,0:T(8,128)S(1)} %get-tuple-element.42.refs_1_.refs_2_.north, f32[4,64,32,128]{3,2,1,0:T(8,128)S(1)} %get-tuple-element.43.refs_2_.refs_3_, ...), custom_call_target="tpu_custom_call" | custom-call | flops 10485760 | tf_op jit(solution)/shard_map/pallas_call | solution.py:363
  30.6 1.8 %collective-permute-start.7 = (f32[32,32,128]{2,1,0:T(8,128)S(1)}, f32[32,32,128]{2,1,0:T(8,128)S(1)}, u32[]{:S(2)}, u32[]{:S(2)}) collective-permute-start(f32[32,32,128]{2,1,0:T(8,128)S(1)} %get-tuple-element.52), channel_id=1, source_target_pairs={{0,4},{4,0},{1,5},{5,1},{2,6},{6,2},{3,7},{7,3},{8,12},{12,8},{9,1... | collective-permute-start | bytes 1572872 | tf_op jit(solution)/shard_map/ppermute | solution.py:36
  32.4 2.2 %shard_map.51 = (f32[4,32,32,128]{3,2,1,0:T(8,128)S(1)}, f32[32,32,128]{2,1,0:T(8,128)S(1)}, f32[4,32,128]{2,1,0:T(8,128)S(1)}, f32[4,64,128]{2,1,0:T(8,128)S(1)}) custom-call(f32[4,64,32,128]{3,2,1,0:T(8,128)S(1)} %get-tuple-element.38.after.refs_0_, f32[4,64,32,128]{3,2,1,0:T(8,128)S(1)} %get-tuple-element.42.refs_1_.refs_2_.north, ...), custom_call_target="tpu_custom_call" | custom-call | flops 10485760 | tf_op jit(solution)/shard_map/pallas_call | solution.py:363
  36.1 2.1 %collective-permute-done.5.refs_5_ = f32[4,32,128]{2,1,0:T(8,128)S(1)} collective-permute-done((f32[4,32,128]{2,1,0:T(8,128)S(1)}, f32[4,32,128]{2,1,0:T(8,128)S(1)}, u32[]{:S(2)}, u32[]{:S(2)}) %collective-permute-start.5) | collective-permute-done | bytes 65568 | tf_op jit(solution)/shard_map/ppermute | solution.py:36
  38.2 6.7 %collective-permute-done.7.refs_7_ = f32[32,32,128]{2,1,0:T(8,128)S(1)} collective-permute-done((f32[32,32,128]{2,1,0:T(8,128)S(1)}, f32[32,32,128]{2,1,0:T(8,128)S(1)}, u32[]{:S(2)}, u32[]{:S(2)}) %collective-permute-start.7) | collective-permute-done | bytes 524320 | tf_op jit(solution)/shard_map/ppermute | solution.py:36
  44.8 2.0 %shard_map.52 = (f32[4,32,32,128]{3,2,1,0:T(8,128)S(1)}, f32[32,32,128]{2,1,0:T(8,128)S(1)}) custom-call(f32[4,32,32,128]{3,2,1,0:T(8,128)S(1)} %get-tuple-element.47.refs_7_.refs_0_, f32[4,32,32,128]{3,2,1,0:T(8,128)S(1)} %get-tuple-element.49.refs_1_, f32[4,64,32,128]{3,2,1,0:T(8,128)S(1)} %get-tuple-element.42.refs_1_.refs_2_.north, ...), custom_call_target="tpu_custom_call" | custom-call | flops 10485760 | tf_op jit(solution)/shard_map/pallas_call | solution.py:363
  46.8 1.5 %collective-permute-start.11 = (f32[32,32,128]{2,1,0:T(8,128)S(1)}, f32[32,32,128]{2,1,0:T(8,128)S(1)}, u32[]{:S(2)}, u32[]{:S(2)}) collective-permute-start(f32[32,32,128]{2,1,0:T(8,128)S(1)} %get-tuple-element.58), channel_id=1, source_target_pairs={{0,4},{4,0},{1,5},{5,1},{2,6},{6,2},{3,7},{7,3},{8,12},{12,8},{9,1... | collective-permute-start | bytes 1572872 | tf_op jit(solution)/shard_map/ppermute | solution.py:36
  48.4 7.7 %collective-permute-done.8.refs_7_ = f32[32,32,128]{2,1,0:T(8,128)S(1)} collective-permute-done((f32[32,32,128]{2,1,0:T(8,128)S(1)}, f32[32,32,128]{2,1,0:T(8,128)S(1)}, u32[]{:S(2)}, u32[]{:S(2)}) %collective-permute-start.8) | collective-permute-done | bytes 524320 | tf_op jit(solution)/shard_map/ppermute | solution.py:36
  56.1 2.2 %shard_map.53 = (f32[4,32,32,128]{3,2,1,0:T(8,128)S(1)}, f32[32,32,128]{2,1,0:T(8,128)S(1)}, f32[4,32,128]{2,1,0:T(8,128)S(1)}, f32[4,64,128]{2,1,0:T(8,128)S(1)}) custom-call(f32[4,32,32,128]{3,2,1,0:T(8,128)S(1)} %get-tuple-element.47.refs_7_.refs_0_, f32[4,32,32,128]{3,2,1,0:T(8,128)S(1)} %get-tuple-element.49.refs_1_, ...), custom_call_target="tpu_custom_call" | custom-call | flops 10485760 | tf_op jit(solution)/shard_map/pallas_call | solution.py:363
  61.0 2.2 %collective-permute-done.9.refs_5_ = f32[4,32,128]{2,1,0:T(8,128)S(1)} collective-permute-done((f32[4,32,128]{2,1,0:T(8,128)S(1)}, f32[4,32,128]{2,1,0:T(8,128)S(1)}, u32[]{:S(2)}, u32[]{:S(2)}) %collective-permute-start.9) | collective-permute-done | bytes 65568 | tf_op jit(solution)/shard_map/ppermute | solution.py:36
  63.2 4.1 %collective-permute-done.11.refs_7_ = f32[32,32,128]{2,1,0:T(8,128)S(1)} collective-permute-done((f32[32,32,128]{2,1,0:T(8,128)S(1)}, f32[32,32,128]{2,1,0:T(8,128)S(1)}, u32[]{:S(2)}, u32[]{:S(2)}) %collective-permute-start.11) | collective-permute-done | bytes 524320 | tf_op jit(solution)/shard_map/ppermute | solution.py:36
  67.3 2.0 %shard_map.54 = (f32[4,32,32,128]{3,2,1,0:T(8,128)S(1)}, f32[32,32,128]{2,1,0:T(8,128)S(1)}) custom-call(f32[4,32,32,128]{3,2,1,0:T(8,128)S(1)} %get-tuple-element.53.refs_8_.refs_0_, f32[4,32,32,128]{3,2,1,0:T(8,128)S(1)} %get-tuple-element.55.refs_1_, f32[4,64,32,128]{3,2,1,0:T(8,128)S(1)} %get-tuple-element.42.refs_1_.refs_2_.north, ...), custom_call_target="tpu_custom_call" | custom-call | flops 10485760 | tf_op jit(solution)/shard_map/pallas_call | solution.py:363
  70.8 7.7 %collective-permute-done.12.refs_7_ = f32[32,32,128]{2,1,0:T(8,128)S(1)} collective-permute-done((f32[32,32,128]{2,1,0:T(8,128)S(1)}, f32[32,32,128]{2,1,0:T(8,128)S(1)}, u32[]{:S(2)}, u32[]{:S(2)}) %collective-permute-start.12) | collective-permute-done | bytes 524320 | tf_op jit(solution)/shard_map/ppermute | solution.py:36
  78.5 2.2 %shard_map.55 = (f32[4,32,32,128]{3,2,1,0:T(8,128)S(1)}, f32[24,32,128]{2,1,0:T(8,128)S(1)}, f32[8,32,128]{2,1,0:T(8,128)S(1)}, f32[4,32,128]{2,1,0:T(8,128)S(1)}, f32[4,64,128]{2,1,0:T(8,128)S(1)}) custom-call(f32[4,32,32,128]{3,2,1,0:T(8,128)S(1)} %get-tuple-element.53.refs_8_.refs_0_, f32[4,32,32,128]{3,2,1,0:T(8,128)S(1)} %get-tuple-element.55.refs_1_, ...), custom_call_target="tpu_custom_call" | custom-call | flops 10485760 | tf_op jit(solution)/shard_map/pallas_call | solution.py:363
  80.7 1.5 %collective-permute-start.16 = (f32[24,32,128]{2,1,0:T(8,128)S(1)}, f32[24,32,128]{2,1,0:T(8,128)S(1)}, u32[]{:S(2)}, u32[]{:S(2)}) collective-permute-start(f32[24,32,128]{2,1,0:T(8,128)S(1)} %get-tuple-element.66), channel_id=1, source_target_pairs={{0,4},{4,0},{1,5},{5,1},{2,6},{6,2},{3,7},{7,3},{8,12},{12,8},{9,1... | collective-permute-start | bytes 1179656 | tf_op jit(solution)/shard_map/ppermute | solution.py:36
  83.7 2.1 %collective-permute-done.13.refs_5_ = f32[4,32,128]{2,1,0:T(8,128)S(1)} collective-permute-done((f32[4,32,128]{2,1,0:T(8,128)S(1)}, f32[4,32,128]{2,1,0:T(8,128)S(1)}, u32[]{:S(2)}, u32[]{:S(2)}) %collective-permute-start.13) | collective-permute-done | bytes 65568 | tf_op jit(solution)/shard_map/ppermute | solution.py:36
  85.8 4.7 %shard_map.56 = (f32[4,64,32,128]{3,2,1,0:T(8,128)}, f32[64,32,128]{2,1,0:T(8,128)S(1)}) custom-call(f32[4,32,32,128]{3,2,1,0:T(8,128)S(1)} %get-tuple-element.59.refs_8_.refs_0_, f32[4,32,32,128]{3,2,1,0:T(8,128)S(1)} %get-tuple-element.61.refs_1_, f32[4,64,32,128]{3,2,1,0:T(8,128)S(1)} %get-tuple-element.42.refs_1_.refs_2_.north, ...), custom_call_target="tpu_custom_call" | custom-call | flops 20971520 | tf_op jit(solution)/shard_map/pallas_call | solution.py:363
  91.4 5.2 %collective-permute-done.16.refs_1_ = f32[24,32,128]{2,1,0:T(8,128)S(1)} collective-permute-done((f32[24,32,128]{2,1,0:T(8,128)S(1)}, f32[24,32,128]{2,1,0:T(8,128)S(1)}, u32[]{:S(2)}, u32[]{:S(2)}) %collective-permute-start.16) | collective-permute-done | bytes 393248 | tf_op jit(solution)/shard_map/ppermute | solution.py:36
  (26 shorter events, 14.2 us)
Async XLA Ops:
  6.8 25.5 %collective-permute-start.4 = (f32[32,32,128]{2,1,0:T(8,128)S(1)}, f32[32,32,128]{2,1,0:T(8,128)S(1)}, u32[]{:S(2)}, u32[]{:S(2)}) collective-permute-start(f32[32,32,128]{2,1,0:T(8,128)S(1)} %get-tuple-element.48), channel_id=1, source_target_pairs={{0,4},{4,0},{1,5},{5,1},{2,6},{6,2},{3,7},{7,3},{8,12},{12,8},{9,1... | collective-permute-start | bytes 1572872 | tf_op jit(solution)/shard_map/ppermute | solution.py:36
  8.9 16.8 %collective-permute-start.2 = (f32[16,32,128]{2,1,0:T(8,128)S(1)}, f32[16,32,128]{2,1,0:T(8,128)S(1)}, u32[]{:S(2)}, u32[]{:S(2)}) collective-permute-start(f32[16,32,128]{2,1,0:T(8,128)S(1)} %shard_map.46.after), channel_id=1, source_target_pairs={{0,4},{4,0},{1,5},{5,1},{2,6},{6,2},{3,7},{7,3},{8,12},{12,8},{9,1... | collective-permute-start | bytes 786440 | tf_op jit(solution)/shard_map/ppermute | solution.py:36
  9.0 19.6 %collective-permute-start.3 = (f32[16,32,128]{2,1,0:T(8,128)S(1)}, f32[16,32,128]{2,1,0:T(8,128)S(1)}, u32[]{:S(2)}, u32[]{:S(2)}) collective-permute-start(f32[16,32,128]{2,1,0:T(8,128)S(1)} %get-tuple-element.37.after), channel_id=1, source_target_pairs={{0,4},{4,0},{1,5},{5,1},{2,6},{6,2},{3,7},{7,3},{8,12},{12,8},{9,1... | collective-permute-start | bytes 786440 | tf_op jit(solution)/shard_map/ppermute | solution.py:36
  12.7 3.6 %collective-permute-start.1 = (f32[4,64,128]{2,1,0:T(8,128)S(1)}, f32[4,64,128]{2,1,0:T(8,128)S(1)}, u32[]{:S(2)}, u32[]{:S(2)}) collective-permute-start(f32[4,64,128]{2,1,0:T(8,128)S(1)} %get-tuple-element.46), channel_id=1, source_target_pairs={{0,1},{1,0},{2,3},{3,2},{4,5},{5,4},{6,7},{7,6},{8,9},{9,8},{10,11... | collective-permute-start | bytes 393224 | tf_op jit(solution)/shard_map/ppermute | solution.py:36
  12.8 3.5 %collective-permute-start = (f32[4,32,128]{2,1,0:T(8,128)S(1)}, f32[4,32,128]{2,1,0:T(8,128)S(1)}, u32[]{:S(2)}, u32[]{:S(2)}) collective-permute-start(f32[4,32,128]{2,1,0:T(8,128)S(1)} %get-tuple-element.45), channel_id=1, source_target_pairs={{0,2},{2,0},{1,3},{3,1},{4,6},{6,4},{5,7},{7,5},{8,10},{10,8},{9,1... | collective-permute-start | bytes 196616 | tf_op jit(solution)/shard_map/ppermute | solution.py:36
  30.6 14.3 %collective-permute-start.7 = (f32[32,32,128]{2,1,0:T(8,128)S(1)}, f32[32,32,128]{2,1,0:T(8,128)S(1)}, u32[]{:S(2)}, u32[]{:S(2)}) collective-permute-start(f32[32,32,128]{2,1,0:T(8,128)S(1)} %get-tuple-element.52), channel_id=1, source_target_pairs={{0,4},{4,0},{1,5},{5,1},{2,6},{6,2},{3,7},{7,3},{8,12},{12,8},{9,1... | collective-permute-start | bytes 1572872 | tf_op jit(solution)/shard_map/ppermute | solution.py:36
  34.5 21.5 %collective-permute-start.8 = (f32[32,32,128]{2,1,0:T(8,128)S(1)}, f32[32,32,128]{2,1,0:T(8,128)S(1)}, u32[]{:S(2)}, u32[]{:S(2)}) collective-permute-start(f32[32,32,128]{2,1,0:T(8,128)S(1)} %get-tuple-element.54), channel_id=1, source_target_pairs={{0,4},{4,0},{1,5},{5,1},{2,6},{6,2},{3,7},{7,3},{8,12},{12,8},{9,1... | collective-permute-start | bytes 1572872 | tf_op jit(solution)/shard_map/ppermute | solution.py:36
  34.6 3.5 %collective-permute-start.6 = (f32[4,64,128]{2,1,0:T(8,128)S(1)}, f32[4,64,128]{2,1,0:T(8,128)S(1)}, u32[]{:S(2)}, u32[]{:S(2)}) collective-permute-start(f32[4,64,128]{2,1,0:T(8,128)S(1)} %get-tuple-element.51), channel_id=1, source_target_pairs={{0,1},{1,0},{2,3},{3,2},{4,5},{5,4},{6,7},{7,6},{8,9},{9,8},{10,11... | collective-permute-start | bytes 393224 | tf_op jit(solution)/shard_map/ppermute | solution.py:36
  34.7 3.5 %collective-permute-start.5 = (f32[4,32,128]{2,1,0:T(8,128)S(1)}, f32[4,32,128]{2,1,0:T(8,128)S(1)}, u32[]{:S(2)}, u32[]{:S(2)}) collective-permute-start(f32[4,32,128]{2,1,0:T(8,128)S(1)} %get-tuple-element.50), channel_id=1, source_target_pairs={{0,2},{2,0},{1,3},{3,1},{4,6},{6,4},{5,7},{7,5},{8,10},{10,8},{9,1... | collective-permute-start | bytes 196616 | tf_op jit(solution)/shard_map/ppermute | solution.py:36
  46.8 20.5 %collective-permute-start.11 = (f32[32,32,128]{2,1,0:T(8,128)S(1)}, f32[32,32,128]{2,1,0:T(8,128)S(1)}, u32[]{:S(2)}, u32[]{:S(2)}) collective-permute-start(f32[32,32,128]{2,1,0:T(8,128)S(1)} %get-tuple-element.58), channel_id=1, source_target_pairs={{0,4},{4,0},{1,5},{5,1},{2,6},{6,2},{3,7},{7,3},{8,12},{12,8},{9,1... | collective-permute-start | bytes 1572872 | tf_op jit(solution)/shard_map/ppermute | solution.py:36
  58.2 20.3 %collective-permute-start.12 = (f32[32,32,128]{2,1,0:T(8,128)S(1)}, f32[32,32,128]{2,1,0:T(8,128)S(1)}, u32[]{:S(2)}, u32[]{:S(2)}) collective-permute-start(f32[32,32,128]{2,1,0:T(8,128)S(1)} %get-tuple-element.60), channel_id=1, source_target_pairs={{0,4},{4,0},{1,5},{5,1},{2,6},{6,2},{3,7},{7,3},{8,12},{12,8},{9,1... | collective-permute-start | bytes 1572872 | tf_op jit(solution)/shard_map/ppermute | solution.py:36
  59.8 3.4 %collective-permute-start.10 = (f32[4,64,128]{2,1,0:T(8,128)S(1)}, f32[4,64,128]{2,1,0:T(8,128)S(1)}, u32[]{:S(2)}, u32[]{:S(2)}) collective-permute-start(f32[4,64,128]{2,1,0:T(8,128)S(1)} %get-tuple-element.57), channel_id=1, source_target_pairs={{0,1},{1,0},{2,3},{3,2},{4,5},{5,4},{6,7},{7,6},{8,9},{9,8},{10,11... | collective-permute-start | bytes 393224 | tf_op jit(solution)/shard_map/ppermute | solution.py:36
  59.8 3.4 %collective-permute-start.9 = (f32[4,32,128]{2,1,0:T(8,128)S(1)}, f32[4,32,128]{2,1,0:T(8,128)S(1)}, u32[]{:S(2)}, u32[]{:S(2)}) collective-permute-start(f32[4,32,128]{2,1,0:T(8,128)S(1)} %get-tuple-element.56), channel_id=1, source_target_pairs={{0,2},{2,0},{1,3},{3,1},{4,6},{6,4},{5,7},{7,5},{8,10},{10,8},{9,1... | collective-permute-start | bytes 196616 | tf_op jit(solution)/shard_map/ppermute | solution.py:36
  69.3 21.2 %collective-permute-start.17 = (f32[32,32,128]{2,1,0:T(8,128)S(1)}, f32[32,32,128]{2,1,0:T(8,128)S(1)}, u32[]{:S(2)}, u32[]{:S(2)}) collective-permute-start(f32[32,32,128]{2,1,0:T(8,128)S(1)} %get-tuple-element.67), channel_id=1, source_target_pairs={{0,4},{4,0},{1,5},{5,1},{2,6},{6,2},{3,7},{7,3},{8,12},{12,8},{9,1... | collective-permute-start | bytes 1572872 | tf_op jit(solution)/shard_map/ppermute | solution.py:36
  80.7 16.0 %collective-permute-start.16 = (f32[24,32,128]{2,1,0:T(8,128)S(1)}, f32[24,32,128]{2,1,0:T(8,128)S(1)}, u32[]{:S(2)}, u32[]{:S(2)}) collective-permute-start(f32[24,32,128]{2,1,0:T(8,128)S(1)} %get-tuple-element.66), channel_id=1, source_target_pairs={{0,4},{4,0},{1,5},{5,1},{2,6},{6,2},{3,7},{7,3},{8,12},{12,8},{9,1... | collective-permute-start | bytes 1179656 | tf_op jit(solution)/shard_map/ppermute | solution.py:36
  82.2 3.6 %collective-permute-start.14 = (f32[4,64,128]{2,1,0:T(8,128)S(1)}, f32[4,64,128]{2,1,0:T(8,128)S(1)}, u32[]{:S(2)}, u32[]{:S(2)}) collective-permute-start(f32[4,64,128]{2,1,0:T(8,128)S(1)} %get-tuple-element.63), channel_id=1, source_target_pairs={{0,1},{1,0},{2,3},{3,2},{4,5},{5,4},{6,7},{7,6},{8,9},{9,8},{10,11... | collective-permute-start | bytes 393224 | tf_op jit(solution)/shard_map/ppermute | solution.py:36
  82.2 15.8 %collective-permute-start.15 = (f32[8,32,128]{2,1,0:T(8,128)S(1)}, f32[8,32,128]{2,1,0:T(8,128)S(1)}, u32[]{:S(2)}, u32[]{:S(2)}) collective-permute-start(f32[8,32,128]{2,1,0:T(8,128)S(1)} %get-tuple-element.65), channel_id=1, source_target_pairs={{0,4},{4,0},{1,5},{5,1},{2,6},{6,2},{3,7},{7,3},{8,12},{12,8},{9,1... | collective-permute-start | bytes 393224 | tf_op jit(solution)/shard_map/ppermute | solution.py:36
  82.4 3.4 %collective-permute-start.13 = (f32[4,32,128]{2,1,0:T(8,128)S(1)}, f32[4,32,128]{2,1,0:T(8,128)S(1)}, u32[]{:S(2)}, u32[]{:S(2)}) collective-permute-start(f32[4,32,128]{2,1,0:T(8,128)S(1)} %get-tuple-element.62), channel_id=1, source_target_pairs={{0,2},{2,0},{1,3},{3,1},{4,6},{6,4},{5,7},{7,5},{8,10},{10,8},{9,1... | collective-permute-start | bytes 196616 | tf_op jit(solution)/shard_map/ppermute | solution.py:36
where the time goes:
time: 99 us; the launch traced here: 98.8 us
  waiting for transfers between devices  52.7 us (53%)
  Pallas kernels  28.7 us (29%)
  starting transfers between devices  17.1 us (17%)
    ppermute x18, waiting for transfers between devices, exchange(): return [lax.ppermute(faces[0], axis, [(0, 1), (1, 0)])]  52.7 us
    pallas_call x14, Pallas kernels, call(): pl.pallas_call(kernel, out_shape=outs, in_specs=in_specs or [in_vmem] * l...  28.7 us
    ppermute x18, starting transfers between devices, exchange(): return [lax.ppermute(faces[0], axis, [(0, 1), (1, 0)])]  17.1 us
  transfers between devices with their start and end apart: 18, of which 12 were waited for; matrix products, arithmetic and copies ran while one was open for 0% of the time, Pallas kernels for 22%

commit v1 on v0

--- a/solution.py
+++ b/solution.py
@@ -97,12 +97,12 @@
     )
 
 
-def load(sources, places, sem, slot, priority=0):
+def load(sources, places, sem, slot):
     copies = [
         pltpu.make_async_copy(source, place, sem.at[slot + i]) for i, (source, place) in enumerate(zip(sources, places))
     ]
     for copy in copies:
-        copy.start(priority=priority)
+        copy.start()
     for copy in copies:
         copy.wait()
 
@@ -117,10 +117,10 @@
 
     def fetch(layers):
         sources = [field.at[layer, pl.ds(start, width)] for start, width in pieces for layer in layers]
-        load(sources, faces, sem, 0, 1 - len(speeds) // 3)
+        load(sources, faces, sem, 0)
 
     if sides == 1:
-        fetch([top * (1 - lax.axis_index("py"))])
+        on_sides("py", lambda: fetch([0]), lambda: fetch([top]))
     else:
         fetch([0, top])
 
@@ -326,23 +326,31 @@
     begin, count = piece
     top = whole.shape[0] - 1
 
+    halves = split(0, count, count // 2)
+
     def finish(layer, sign, side):
-        def run():
-            for x in range(count):
+        copies = []
+        for slot, (first, rows) in enumerate(halves):
+            for x in range(first, first + rows):
                 rate = RATE + sign * north[layer, begin + x]
                 held[side][x] = waiting[side][begin + x] + rate * halo[side][x]
-            copy = pltpu.make_async_copy(held[side], whole.at[layer, pl.ds(begin, count)], sem.at[side])
-            copy.start(priority=1)
+            copies.append(
+                pltpu.make_async_copy(
+                    held[side].at[pl.ds(first, rows)],
+                    whole.at[layer, pl.ds(begin + first, rows)],
+                    sem.at[side * len(halves) + slot],
+                )
+            )
+            copies[-1].start()
+        for copy in copies:
             copy.wait()
 
-        return run
-
-    low, high = finish(0, 1.0, 0), finish(top, -1.0, sides - 1)
     if sides == 1:
-        on_sides("py", low, high)
+        place = lax.axis_index("py")
+        finish(top * (1 - place), (2 * place - 1).astype(jnp.float32), 0)
     else:
-        low()
-        high()
+        finish(0, 1.0, 0)
+        finish(top, -1.0, 1)
 
 
 def body(field, north, east, upward):
@@ -473,7 +481,7 @@
                 flops=3 * piece[1] * nz * lanes,
                 out_specs=[anywhere],
                 input_output_aliases={len(ins) - 1: 0},
-                scratch_shapes=[vmem(piece[1], nz, lanes)] * sides[0] + [dma((sides[0],))],
+                scratch_shapes=[vmem(piece[1], nz, lanes)] * sides[0] + [dma((2 * sides[0],))],
             )
     return whole
 

time: 99 us -> 99 us (level)
  transfers between devices with their start and end apart: 18 -> 18, of which waited for: 12 -> 12; matrix products, arithmetic and copies ran while one was open for 0% -> 0% of each run, Pallas kernels for 22% -> 21%
where the time goes in v1:
time: 99 us; the launch traced here: 98.8 us
  waiting for transfers between devices  52.8 us (53%)
  Pallas kernels  28.7 us (29%)
  starting transfers between devices  17.2 us (17%)
    ppermute x18, waiting for transfers between devices, exchange(): return [lax.ppermute(faces[0], axis, [(0, 1), (1, 0)])]  52.8 us
    pallas_call x14, Pallas kernels, call(): pl.pallas_call(kernel, out_shape=outs, in_specs=in_specs or [in_vmem] * l...  28.7 us
    ppermute x18, starting transfers between devices, exchange(): return [lax.ppermute(faces[0], axis, [(0, 1), (1, 0)])]  17.2 us
  transfers between devices with their start and end apart: 18, of which 12 were waited for; matrix products, arithmetic and copies ran while one was open for 0% of the time, Pallas kernels for 21%

profile of v1, /device:TPU:1, one launch (start us, length us, event | category | flops | bytes accessed | tf_op | source)
XLA Modules:
  0.0 98.8 jit_solution(15162835609565831682)
XLA Ops:
  1.0 5.8 %shard_map.47 = (f32[16,32,128]{2,1,0:T(8,128)S(1)}, f32[32,32,128]{2,1,0:T(8,128)S(1)}, f32[4,64,32,128]{3,2,1,0:T(8,128)S(1)}, f32[4,64,32,128]{3,2,1,0:T(8,128)S(1)}, f32[4,64,32,128]{3,2,1,0:T(8,128)S(1)}) custom-call(f32[4,64,32,128]{3,2,1,0:T(8,128)} %field.5, f32[16,32,128]{2,1,0:T(8,128)S(1)} %shard_map.46.after, f32[4,64,32,128]{3,2,1,0:T(8,128)} %north.1, ...), custom_call_target="tpu_custom_call" | custom-call | flops 1000000 | tf_op jit(solution)/shard_map/pallas_call | solution.py:371
  6.8 2.1 %collective-permute-start.4 = (f32[32,32,128]{2,1,0:T(8,128)S(1)}, f32[32,32,128]{2,1,0:T(8,128)S(1)}, u32[]{:S(2)}, u32[]{:S(2)}) collective-permute-start(f32[32,32,128]{2,1,0:T(8,128)S(1)} %get-tuple-element.48), channel_id=1, source_target_pairs={{0,4},{4,0},{1,5},{5,1},{2,6},{6,2},{3,7},{7,3},{8,12},{12,8},{9,1... | collective-permute-start | bytes 1572872 | tf_op jit(solution)/shard_map/ppermute | solution.py:36
  10.4 2.3 %shard_map.48 = (f32[4,64,32,128]{3,2,1,0:T(8,128)S(1)}, f32[4,32,128]{2,1,0:T(8,128)S(1)}, f32[4,64,128]{2,1,0:T(8,128)S(1)}) custom-call(f32[4,64,32,128]{3,2,1,0:T(8,128)} %field.5, f32[16,32,128]{2,1,0:T(8,128)S(1)} %get-tuple-element.37.after), custom_call_target="tpu_custom_call" | custom-call | flops 1000000 | tf_op jit(solution)/shard_map/pallas_call | solution.py:371
  14.1 2.1 %collective-permute-done.refs_4_ = f32[4,32,128]{2,1,0:T(8,128)S(1)} collective-permute-done((f32[4,32,128]{2,1,0:T(8,128)S(1)}, f32[4,32,128]{2,1,0:T(8,128)S(1)}, u32[]{:S(2)}, u32[]{:S(2)}) %collective-permute-start) | collective-permute-done | bytes 65568 | tf_op jit(solution)/shard_map/ppermute | solution.py:36
  16.3 9.5 %collective-permute-done.2.refs_6_ = f32[16,32,128]{2,1,0:T(8,128)S(1)} collective-permute-done((f32[16,32,128]{2,1,0:T(8,128)S(1)}, f32[16,32,128]{2,1,0:T(8,128)S(1)}, u32[]{:S(2)}, u32[]{:S(2)}) %collective-permute-start.2) | collective-permute-done | bytes 262176 | tf_op jit(solution)/shard_map/ppermute | solution.py:36
  25.7 2.8 %collective-permute-done.3.refs_7_ = f32[16,32,128]{2,1,0:T(8,128)S(1)} collective-permute-done((f32[16,32,128]{2,1,0:T(8,128)S(1)}, f32[16,32,128]{2,1,0:T(8,128)S(1)}, u32[]{:S(2)}, u32[]{:S(2)}) %collective-permute-start.3) | collective-permute-done | bytes 262176 | tf_op jit(solution)/shard_map/ppermute | solution.py:36
  28.5 2.0 %shard_map.50 = (f32[4,32,32,128]{3,2,1,0:T(8,128)S(1)}, f32[32,32,128]{2,1,0:T(8,128)S(1)}) custom-call(f32[4,64,32,128]{3,2,1,0:T(8,128)S(1)} %get-tuple-element.38.after.refs_0_, f32[4,64,32,128]{3,2,1,0:T(8,128)S(1)} %get-tuple-element.42.refs_1_.refs_2_.north, f32[4,64,32,128]{3,2,1,0:T(8,128)S(1)} %get-tuple-element.43.refs_2_.refs_3_, ...), custom_call_target="tpu_custom_call" | custom-call | flops 10485760 | tf_op jit(solution)/shard_map/pallas_call | solution.py:371
  30.6 1.8 %collective-permute-start.7 = (f32[32,32,128]{2,1,0:T(8,128)S(1)}, f32[32,32,128]{2,1,0:T(8,128)S(1)}, u32[]{:S(2)}, u32[]{:S(2)}) collective-permute-start(f32[32,32,128]{2,1,0:T(8,128)S(1)} %get-tuple-element.52), channel_id=1, source_target_pairs={{0,4},{4,0},{1,5},{5,1},{2,6},{6,2},{3,7},{7,3},{8,12},{12,8},{9,1... | collective-permute-start | bytes 1572872 | tf_op jit(solution)/shard_map/ppermute | solution.py:36
  32.4 2.2 %shard_map.51 = (f32[4,32,32,128]{3,2,1,0:T(8,128)S(1)}, f32[32,32,128]{2,1,0:T(8,128)S(1)}, f32[4,32,128]{2,1,0:T(8,128)S(1)}, f32[4,64,128]{2,1,0:T(8,128)S(1)}) custom-call(f32[4,64,32,128]{3,2,1,0:T(8,128)S(1)} %get-tuple-element.38.after.refs_0_, f32[4,64,32,128]{3,2,1,0:T(8,128)S(1)} %get-tuple-element.42.refs_1_.refs_2_.north, ...), custom_call_target="tpu_custom_call" | custom-call | flops 10485760 | tf_op jit(solution)/shard_map/pallas_call | solution.py:371
  36.1 2.1 %collective-permute-done.5.refs_5_ = f32[4,32,128]{2,1,0:T(8,128)S(1)} collective-permute-done((f32[4,32,128]{2,1,0:T(8,128)S(1)}, f32[4,32,128]{2,1,0:T(8,128)S(1)}, u32[]{:S(2)}, u32[]{:S(2)}) %collective-permute-start.5) | collective-permute-done | bytes 65568 | tf_op jit(solution)/shard_map/ppermute | solution.py:36
  38.2 6.7 %collective-permute-done.7.refs_7_ = f32[32,32,128]{2,1,0:T(8,128)S(1)} collective-permute-done((f32[32,32,128]{2,1,0:T(8,128)S(1)}, f32[32,32,128]{2,1,0:T(8,128)S(1)}, u32[]{:S(2)}, u32[]{:S(2)}) %collective-permute-start.7) | collective-permute-done | bytes 524320 | tf_op jit(solution)/shard_map/ppermute | solution.py:36
  44.8 2.0 %shard_map.52 = (f32[4,32,32,128]{3,2,1,0:T(8,128)S(1)}, f32[32,32,128]{2,1,0:T(8,128)S(1)}) custom-call(f32[4,32,32,128]{3,2,1,0:T(8,128)S(1)} %get-tuple-element.47.refs_7_.refs_0_, f32[4,32,32,128]{3,2,1,0:T(8,128)S(1)} %get-tuple-element.49.refs_1_, f32[4,64,32,128]{3,2,1,0:T(8,128)S(1)} %get-tuple-element.42.refs_1_.refs_2_.north, ...), custom_call_target="tpu_custom_call" | custom-call | flops 10485760 | tf_op jit(solution)/shard_map/pallas_call | solution.py:371
  48.4 7.7 %collective-permute-done.8.refs_7_ = f32[32,32,128]{2,1,0:T(8,128)S(1)} collective-permute-done((f32[32,32,128]{2,1,0:T(8,128)S(1)}, f32[32,32,128]{2,1,0:T(8,128)S(1)}, u32[]{:S(2)}, u32[]{:S(2)}) %collective-permute-start.8) | collective-permute-done | bytes 524320 | tf_op jit(solution)/shard_map/ppermute | solution.py:36
  56.1 2.2 %shard_map.53 = (f32[4,32,32,128]{3,2,1,0:T(8,128)S(1)}, f32[32,32,128]{2,1,0:T(8,128)S(1)}, f32[4,32,128]{2,1,0:T(8,128)S(1)}, f32[4,64,128]{2,1,0:T(8,128)S(1)}) custom-call(f32[4,32,32,128]{3,2,1,0:T(8,128)S(1)} %get-tuple-element.47.refs_7_.refs_0_, f32[4,32,32,128]{3,2,1,0:T(8,128)S(1)} %get-tuple-element.49.refs_1_, ...), custom_call_target="tpu_custom_call" | custom-call | flops 10485760 | tf_op jit(solution)/shard_map/pallas_call | solution.py:371
  58.2 1.5 %collective-permute-start.12 = (f32[32,32,128]{2,1,0:T(8,128)S(1)}, f32[32,32,128]{2,1,0:T(8,128)S(1)}, u32[]{:S(2)}, u32[]{:S(2)}) collective-permute-start(f32[32,32,128]{2,1,0:T(8,128)S(1)} %get-tuple-element.60), channel_id=1, source_target_pairs={{0,4},{4,0},{1,5},{5,1},{2,6},{6,2},{3,7},{7,3},{8,12},{12,8},{9,1... | collective-permute-start | bytes 1572872 | tf_op jit(solution)/shard_map/ppermute | solution.py:36
  61.0 2.2 %collective-permute-done.9.refs_5_ = f32[4,32,128]{2,1,0:T(8,128)S(1)} collective-permute-done((f32[4,32,128]{2,1,0:T(8,128)S(1)}, f32[4,32,128]{2,1,0:T(8,128)S(1)}, u32[]{:S(2)}, u32[]{:S(2)}) %collective-permute-start.9) | collective-permute-done | bytes 65568 | tf_op jit(solution)/shard_map/ppermute | solution.py:36
  63.2 4.1 %collective-permute-done.11.refs_7_ = f32[32,32,128]{2,1,0:T(8,128)S(1)} collective-permute-done((f32[32,32,128]{2,1,0:T(8,128)S(1)}, f32[32,32,128]{2,1,0:T(8,128)S(1)}, u32[]{:S(2)}, u32[]{:S(2)}) %collective-permute-start.11) | collective-permute-done | bytes 524320 | tf_op jit(solution)/shard_map/ppermute | solution.py:36
  67.3 2.0 %shard_map.54 = (f32[4,32,32,128]{3,2,1,0:T(8,128)S(1)}, f32[32,32,128]{2,1,0:T(8,128)S(1)}) custom-call(f32[4,32,32,128]{3,2,1,0:T(8,128)S(1)} %get-tuple-element.53.refs_8_.refs_0_, f32[4,32,32,128]{3,2,1,0:T(8,128)S(1)} %get-tuple-element.55.refs_1_, f32[4,64,32,128]{3,2,1,0:T(8,128)S(1)} %get-tuple-element.42.refs_1_.refs_2_.north, ...), custom_call_target="tpu_custom_call" | custom-call | flops 10485760 | tf_op jit(solution)/shard_map/pallas_call | solution.py:371
  69.3 1.5 %collective-permute-start.17 = (f32[32,32,128]{2,1,0:T(8,128)S(1)}, f32[32,32,128]{2,1,0:T(8,128)S(1)}, u32[]{:S(2)}, u32[]{:S(2)}) collective-permute-start(f32[32,32,128]{2,1,0:T(8,128)S(1)} %get-tuple-element.67), channel_id=1, source_target_pairs={{0,4},{4,0},{1,5},{5,1},{2,6},{6,2},{3,7},{7,3},{8,12},{12,8},{9,1... | collective-permute-start | bytes 1572872 | tf_op jit(solution)/shard_map/ppermute | solution.py:36
  70.8 7.7 %collective-permute-done.12.refs_7_ = f32[32,32,128]{2,1,0:T(8,128)S(1)} collective-permute-done((f32[32,32,128]{2,1,0:T(8,128)S(1)}, f32[32,32,128]{2,1,0:T(8,128)S(1)}, u32[]{:S(2)}, u32[]{:S(2)}) %collective-permute-start.12) | collective-permute-done | bytes 524320 | tf_op jit(solution)/shard_map/ppermute | solution.py:36
  78.5 2.2 %shard_map.55 = (f32[4,32,32,128]{3,2,1,0:T(8,128)S(1)}, f32[24,32,128]{2,1,0:T(8,128)S(1)}, f32[8,32,128]{2,1,0:T(8,128)S(1)}, f32[4,32,128]{2,1,0:T(8,128)S(1)}, f32[4,64,128]{2,1,0:T(8,128)S(1)}) custom-call(f32[4,32,32,128]{3,2,1,0:T(8,128)S(1)} %get-tuple-element.53.refs_8_.refs_0_, f32[4,32,32,128]{3,2,1,0:T(8,128)S(1)} %get-tuple-element.55.refs_1_, ...), custom_call_target="tpu_custom_call" | custom-call | flops 10485760 | tf_op jit(solution)/shard_map/pallas_call | solution.py:371
  83.7 2.1 %collective-permute-done.13.refs_5_ = f32[4,32,128]{2,1,0:T(8,128)S(1)} collective-permute-done((f32[4,32,128]{2,1,0:T(8,128)S(1)}, f32[4,32,128]{2,1,0:T(8,128)S(1)}, u32[]{:S(2)}, u32[]{:S(2)}) %collective-permute-start.13) | collective-permute-done | bytes 65568 | tf_op jit(solution)/shard_map/ppermute | solution.py:36
  85.8 4.7 %shard_map.56 = (f32[4,64,32,128]{3,2,1,0:T(8,128)}, f32[64,32,128]{2,1,0:T(8,128)S(1)}) custom-call(f32[4,32,32,128]{3,2,1,0:T(8,128)S(1)} %get-tuple-element.59.refs_8_.refs_0_, f32[4,32,32,128]{3,2,1,0:T(8,128)S(1)} %get-tuple-element.61.refs_1_, f32[4,64,32,128]{3,2,1,0:T(8,128)S(1)} %get-tuple-element.42.refs_1_.refs_2_.north, ...), custom_call_target="tpu_custom_call" | custom-call | flops 20971520 | tf_op jit(solution)/shard_map/pallas_call | solution.py:371
  91.4 5.3 %collective-permute-done.16.refs_1_ = f32[24,32,128]{2,1,0:T(8,128)S(1)} collective-permute-done((f32[24,32,128]{2,1,0:T(8,128)S(1)}, f32[24,32,128]{2,1,0:T(8,128)S(1)}, u32[]{:S(2)}, u32[]{:S(2)}) %collective-permute-start.16) | collective-permute-done | bytes 393248 | tf_op jit(solution)/shard_map/ppermute | solution.py:36
  (26 shorter events, 14.1 us)
Async XLA Ops:
  6.8 25.5 %collective-permute-start.4 = (f32[32,32,128]{2,1,0:T(8,128)S(1)}, f32[32,32,128]{2,1,0:T(8,128)S(1)}, u32[]{:S(2)}, u32[]{:S(2)}) collective-permute-start(f32[32,32,128]{2,1,0:T(8,128)S(1)} %get-tuple-element.48), channel_id=1, source_target_pairs={{0,4},{4,0},{1,5},{5,1},{2,6},{6,2},{3,7},{7,3},{8,12},{12,8},{9,1... | collective-permute-start | bytes 1572872 | tf_op jit(solution)/shard_map/ppermute | solution.py:36
  8.9 16.8 %collective-permute-start.2 = (f32[16,32,128]{2,1,0:T(8,128)S(1)}, f32[16,32,128]{2,1,0:T(8,128)S(1)}, u32[]{:S(2)}, u32[]{:S(2)}) collective-permute-start(f32[16,32,128]{2,1,0:T(8,128)S(1)} %shard_map.46.after), channel_id=1, source_target_pairs={{0,4},{4,0},{1,5},{5,1},{2,6},{6,2},{3,7},{7,3},{8,12},{12,8},{9,1... | collective-permute-start | bytes 786440 | tf_op jit(solution)/shard_map/ppermute | solution.py:36
  9.0 19.6 %collective-permute-start.3 = (f32[16,32,128]{2,1,0:T(8,128)S(1)}, f32[16,32,128]{2,1,0:T(8,128)S(1)}, u32[]{:S(2)}, u32[]{:S(2)}) collective-permute-start(f32[16,32,128]{2,1,0:T(8,128)S(1)} %get-tuple-element.37.after), channel_id=1, source_target_pairs={{0,4},{4,0},{1,5},{5,1},{2,6},{6,2},{3,7},{7,3},{8,12},{12,8},{9,1... | collective-permute-start | bytes 786440 | tf_op jit(solution)/shard_map/ppermute | solution.py:36
  12.7 3.6 %collective-permute-start.1 = (f32[4,64,128]{2,1,0:T(8,128)S(1)}, f32[4,64,128]{2,1,0:T(8,128)S(1)}, u32[]{:S(2)}, u32[]{:S(2)}) collective-permute-start(f32[4,64,128]{2,1,0:T(8,128)S(1)} %get-tuple-element.46), channel_id=1, source_target_pairs={{0,1},{1,0},{2,3},{3,2},{4,5},{5,4},{6,7},{7,6},{8,9},{9,8},{10,11... | collective-permute-start | bytes 393224 | tf_op jit(solution)/shard_map/ppermute | solution.py:36
  12.8 3.5 %collective-permute-start = (f32[4,32,128]{2,1,0:T(8,128)S(1)}, f32[4,32,128]{2,1,0:T(8,128)S(1)}, u32[]{:S(2)}, u32[]{:S(2)}) collective-permute-start(f32[4,32,128]{2,1,0:T(8,128)S(1)} %get-tuple-element.45), channel_id=1, source_target_pairs={{0,2},{2,0},{1,3},{3,1},{4,6},{6,4},{5,7},{7,5},{8,10},{10,8},{9,1... | collective-permute-start | bytes 196616 | tf_op jit(solution)/shard_map/ppermute | solution.py:36
  30.6 14.3 %collective-permute-start.7 = (f32[32,32,128]{2,1,0:T(8,128)S(1)}, f32[32,32,128]{2,1,0:T(8,128)S(1)}, u32[]{:S(2)}, u32[]{:S(2)}) collective-permute-start(f32[32,32,128]{2,1,0:T(8,128)S(1)} %get-tuple-element.52), channel_id=1, source_target_pairs={{0,4},{4,0},{1,5},{5,1},{2,6},{6,2},{3,7},{7,3},{8,12},{12,8},{9,1... | collective-permute-start | bytes 1572872 | tf_op jit(solution)/shard_map/ppermute | solution.py:36
  34.5 21.5 %collective-permute-start.8 = (f32[32,32,128]{2,1,0:T(8,128)S(1)}, f32[32,32,128]{2,1,0:T(8,128)S(1)}, u32[]{:S(2)}, u32[]{:S(2)}) collective-permute-start(f32[32,32,128]{2,1,0:T(8,128)S(1)} %get-tuple-element.54), channel_id=1, source_target_pairs={{0,4},{4,0},{1,5},{5,1},{2,6},{6,2},{3,7},{7,3},{8,12},{12,8},{9,1... | collective-permute-start | bytes 1572872 | tf_op jit(solution)/shard_map/ppermute | solution.py:36
  34.6 3.5 %collective-permute-start.6 = (f32[4,64,128]{2,1,0:T(8,128)S(1)}, f32[4,64,128]{2,1,0:T(8,128)S(1)}, u32[]{:S(2)}, u32[]{:S(2)}) collective-permute-start(f32[4,64,128]{2,1,0:T(8,128)S(1)} %get-tuple-element.51), channel_id=1, source_target_pairs={{0,1},{1,0},{2,3},{3,2},{4,5},{5,4},{6,7},{7,6},{8,9},{9,8},{10,11... | collective-permute-start | bytes 393224 | tf_op jit(solution)/shard_map/ppermute | solution.py:36
  34.7 3.5 %collective-permute-start.5 = (f32[4,32,128]{2,1,0:T(8,128)S(1)}, f32[4,32,128]{2,1,0:T(8,128)S(1)}, u32[]{:S(2)}, u32[]{:S(2)}) collective-permute-start(f32[4,32,128]{2,1,0:T(8,128)S(1)} %get-tuple-element.50), channel_id=1, source_target_pairs={{0,2},{2,0},{1,3},{3,1},{4,6},{6,4},{5,7},{7,5},{8,10},{10,8},{9,1... | collective-permute-start | bytes 196616 | tf_op jit(solution)/shard_map/ppermute | solution.py:36
  46.8 20.5 %collective-permute-start.11 = (f32[32,32,128]{2,1,0:T(8,128)S(1)}, f32[32,32,128]{2,1,0:T(8,128)S(1)}, u32[]{:S(2)}, u32[]{:S(2)}) collective-permute-start(f32[32,32,128]{2,1,0:T(8,128)S(1)} %get-tuple-element.58), channel_id=1, source_target_pairs={{0,4},{4,0},{1,5},{5,1},{2,6},{6,2},{3,7},{7,3},{8,12},{12,8},{9,1... | collective-permute-start | bytes 1572872 | tf_op jit(solution)/shard_map/ppermute | solution.py:36
  58.2 20.3 %collective-permute-start.12 = (f32[32,32,128]{2,1,0:T(8,128)S(1)}, f32[32,32,128]{2,1,0:T(8,128)S(1)}, u32[]{:S(2)}, u32[]{:S(2)}) collective-permute-start(f32[32,32,128]{2,1,0:T(8,128)S(1)} %get-tuple-element.60), channel_id=1, source_target_pairs={{0,4},{4,0},{1,5},{5,1},{2,6},{6,2},{3,7},{7,3},{8,12},{12,8},{9,1... | collective-permute-start | bytes 1572872 | tf_op jit(solution)/shard_map/ppermute | solution.py:36
  59.8 3.4 %collective-permute-start.10 = (f32[4,64,128]{2,1,0:T(8,128)S(1)}, f32[4,64,128]{2,1,0:T(8,128)S(1)}, u32[]{:S(2)}, u32[]{:S(2)}) collective-permute-start(f32[4,64,128]{2,1,0:T(8,128)S(1)} %get-tuple-element.57), channel_id=1, source_target_pairs={{0,1},{1,0},{2,3},{3,2},{4,5},{5,4},{6,7},{7,6},{8,9},{9,8},{10,11... | collective-permute-start | bytes 393224 | tf_op jit(solution)/shard_map/ppermute | solution.py:36
  59.8 3.4 %collective-permute-start.9 = (f32[4,32,128]{2,1,0:T(8,128)S(1)}, f32[4,32,128]{2,1,0:T(8,128)S(1)}, u32[]{:S(2)}, u32[]{:S(2)}) collective-permute-start(f32[4,32,128]{2,1,0:T(8,128)S(1)} %get-tuple-element.56), channel_id=1, source_target_pairs={{0,2},{2,0},{1,3},{3,1},{4,6},{6,4},{5,7},{7,5},{8,10},{10,8},{9,1... | collective-permute-start | bytes 196616 | tf_op jit(solution)/shard_map/ppermute | solution.py:36
  69.3 21.2 %collective-permute-start.17 = (f32[32,32,128]{2,1,0:T(8,128)S(1)}, f32[32,32,128]{2,1,0:T(8,128)S(1)}, u32[]{:S(2)}, u32[]{:S(2)}) collective-permute-start(f32[32,32,128]{2,1,0:T(8,128)S(1)} %get-tuple-element.67), channel_id=1, source_target_pairs={{0,4},{4,0},{1,5},{5,1},{2,6},{6,2},{3,7},{7,3},{8,12},{12,8},{9,1... | collective-permute-start | bytes 1572872 | tf_op jit(solution)/shard_map/ppermute | solution.py:36
  80.7 16.0 %collective-permute-start.16 = (f32[24,32,128]{2,1,0:T(8,128)S(1)}, f32[24,32,128]{2,1,0:T(8,128)S(1)}, u32[]{:S(2)}, u32[]{:S(2)}) collective-permute-start(f32[24,32,128]{2,1,0:T(8,128)S(1)} %get-tuple-element.66), channel_id=1, source_target_pairs={{0,4},{4,0},{1,5},{5,1},{2,6},{6,2},{3,7},{7,3},{8,12},{12,8},{9,1... | collective-permute-start | bytes 1179656 | tf_op jit(solution)/shard_map/ppermute | solution.py:36
  82.2 3.6 %collective-permute-start.14 = (f32[4,64,128]{2,1,0:T(8,128)S(1)}, f32[4,64,128]{2,1,0:T(8,128)S(1)}, u32[]{:S(2)}, u32[]{:S(2)}) collective-permute-start(f32[4,64,128]{2,1,0:T(8,128)S(1)} %get-tuple-element.63), channel_id=1, source_target_pairs={{0,1},{1,0},{2,3},{3,2},{4,5},{5,4},{6,7},{7,6},{8,9},{9,8},{10,11... | collective-permute-start | bytes 393224 | tf_op jit(solution)/shard_map/ppermute | solution.py:36
  82.2 15.8 %collective-permute-start.15 = (f32[8,32,128]{2,1,0:T(8,128)S(1)}, f32[8,32,128]{2,1,0:T(8,128)S(1)}, u32[]{:S(2)}, u32[]{:S(2)}) collective-permute-start(f32[8,32,128]{2,1,0:T(8,128)S(1)} %get-tuple-element.65), channel_id=1, source_target_pairs={{0,4},{4,0},{1,5},{5,1},{2,6},{6,2},{3,7},{7,3},{8,12},{12,8},{9,1... | collective-permute-start | bytes 393224 | tf_op jit(solution)/shard_map/ppermute | solution.py:36
  82.4 3.4 %collective-permute-start.13 = (f32[4,32,128]{2,1,0:T(8,128)S(1)}, f32[4,32,128]{2,1,0:T(8,128)S(1)}, u32[]{:S(2)}, u32[]{:S(2)}) collective-permute-start(f32[4,32,128]{2,1,0:T(8,128)S(1)} %get-tuple-element.62), channel_id=1, source_target_pairs={{0,2},{2,0},{1,3},{3,1},{4,6},{6,4},{5,7},{7,5},{8,10},{10,8},{9,1... | collective-permute-start | bytes 196616 | tf_op jit(solution)/shard_map/ppermute | solution.py:36

commit v2 on v0

--- a/solution.py
+++ b/solution.py
@@ -12,7 +12,7 @@
 RATE = 0.05
 CHUNKS = 2
 ROWS = 8
-FIRST = 16
+FIRST = 12
 VMEM = pltpu.VMEM
 
 
@@ -97,12 +97,12 @@
     )
 
 
-def load(sources, places, sem, slot, priority=0):
+def load(sources, places, sem, slot):
     copies = [
         pltpu.make_async_copy(source, place, sem.at[slot + i]) for i, (source, place) in enumerate(zip(sources, places))
     ]
     for copy in copies:
-        copy.start(priority=priority)
+        copy.start()
     for copy in copies:
         copy.wait()
 
@@ -117,10 +117,10 @@
 
     def fetch(layers):
         sources = [field.at[layer, pl.ds(start, width)] for start, width in pieces for layer in layers]
-        load(sources, faces, sem, 0, 1 - len(speeds) // 3)
+        load(sources, faces, sem, 0)
 
     if sides == 1:
-        fetch([top * (1 - lax.axis_index("py"))])
+        on_sides("py", lambda: fetch([0]), lambda: fetch([top]))
     else:
         fetch([0, top])
 
@@ -332,7 +332,7 @@
                 rate = RATE + sign * north[layer, begin + x]
                 held[side][x] = waiting[side][begin + x] + rate * halo[side][x]
             copy = pltpu.make_async_copy(held[side], whole.at[layer, pl.ds(begin, count)], sem.at[side])
-            copy.start(priority=1)
+            copy.start()
             copy.wait()
 
         return run

time: 99 us -> 98.9 us (level)
  transfers between devices with their start and end apart: 18 -> 18, of which waited for: 12 -> 11; matrix products, arithmetic and copies ran while one was open for 0% -> 0% of each run, Pallas kernels for 22% -> 22%
where the time goes in v2:
time: 98.9 us; the launch traced here: 98.8 us
  waiting for transfers between devices  52.7 us (53%)
  Pallas kernels  28.7 us (29%)
  starting transfers between devices  17.2 us (17%)
    ppermute x18, waiting for transfers between devices, exchange(): return [lax.ppermute(faces[0], axis, [(0, 1), (1, 0)])]  52.7 us
    pallas_call x14, Pallas kernels, call(): pl.pallas_call(kernel, out_shape=outs, in_specs=in_specs or [in_vmem] * l...  28.7 us
    ppermute x18, starting transfers between devices, exchange(): return [lax.ppermute(faces[0], axis, [(0, 1), (1, 0)])]  17.2 us
  transfers between devices with their start and end apart: 18, of which 11 were waited for; matrix products, arithmetic and copies ran while one was open for 0% of the time, Pallas kernels for 22%

profile of v2, /device:TPU:1, one launch (start us, length us, event | category | flops | bytes accessed | tf_op | source)
XLA Modules:
  0.0 98.8 jit_solution(7224735770041177055)
XLA Ops:
  0.9 5.9 %shard_map.47 = (f32[20,32,128]{2,1,0:T(8,128)S(1)}, f32[32,32,128]{2,1,0:T(8,128)S(1)}, f32[4,64,32,128]{3,2,1,0:T(8,128)S(1)}, f32[4,64,32,128]{3,2,1,0:T(8,128)S(1)}, f32[4,64,32,128]{3,2,1,0:T(8,128)S(1)}) custom-call(f32[4,64,32,128]{3,2,1,0:T(8,128)} %field.5, f32[12,32,128]{2,1,0:T(8,128)S(1)} %shard_map.46.after, f32[4,64,32,128]{3,2,1,0:T(8,128)} %north.1, ...), custom_call_target="tpu_custom_call" | custom-call | flops 1000000 | tf_op jit(solution)/shard_map/pallas_call | solution.py:363
  6.8 2.1 %collective-permute-start.4 = (f32[32,32,128]{2,1,0:T(8,128)S(1)}, f32[32,32,128]{2,1,0:T(8,128)S(1)}, u32[]{:S(2)}, u32[]{:S(2)}) collective-permute-start(f32[32,32,128]{2,1,0:T(8,128)S(1)} %get-tuple-element.48), channel_id=1, source_target_pairs={{0,4},{4,0},{1,5},{5,1},{2,6},{6,2},{3,7},{7,3},{8,12},{12,8},{9,1... | collective-permute-start | bytes 1572872 | tf_op jit(solution)/shard_map/ppermute | solution.py:36
  10.4 2.3 %shard_map.48 = (f32[4,64,32,128]{3,2,1,0:T(8,128)S(1)}, f32[4,32,128]{2,1,0:T(8,128)S(1)}, f32[4,64,128]{2,1,0:T(8,128)S(1)}) custom-call(f32[4,64,32,128]{3,2,1,0:T(8,128)} %field.5, f32[20,32,128]{2,1,0:T(8,128)S(1)} %get-tuple-element.37.after), custom_call_target="tpu_custom_call" | custom-call | flops 1000000 | tf_op jit(solution)/shard_map/pallas_call | solution.py:363
  14.1 2.1 %collective-permute-done.refs_4_ = f32[4,32,128]{2,1,0:T(8,128)S(1)} collective-permute-done((f32[4,32,128]{2,1,0:T(8,128)S(1)}, f32[4,32,128]{2,1,0:T(8,128)S(1)}, u32[]{:S(2)}, u32[]{:S(2)}) %collective-permute-start) | collective-permute-done | bytes 65568 | tf_op jit(solution)/shard_map/ppermute | solution.py:36
  16.3 12.3 %collective-permute-done.2.refs_6_ = f32[12,32,128]{2,1,0:T(8,128)S(1)} collective-permute-done((f32[12,32,128]{2,1,0:T(8,128)S(1)}, f32[12,32,128]{2,1,0:T(8,128)S(1)}, u32[]{:S(2)}, u32[]{:S(2)}) %collective-permute-start.2) | collective-permute-done | bytes 196640 | tf_op jit(solution)/shard_map/ppermute | solution.py:36
  28.5 2.0 %shard_map.50 = (f32[4,32,32,128]{3,2,1,0:T(8,128)S(1)}, f32[32,32,128]{2,1,0:T(8,128)S(1)}) custom-call(f32[4,64,32,128]{3,2,1,0:T(8,128)S(1)} %get-tuple-element.38.after.refs_0_, f32[4,64,32,128]{3,2,1,0:T(8,128)S(1)} %get-tuple-element.42.refs_1_.refs_2_.north, f32[4,64,32,128]{3,2,1,0:T(8,128)S(1)} %get-tuple-element.43.refs_2_.refs_3_, ...), custom_call_target="tpu_custom_call" | custom-call | flops 10485760 | tf_op jit(solution)/shard_map/pallas_call | solution.py:363
  30.6 1.8 %collective-permute-start.7 = (f32[32,32,128]{2,1,0:T(8,128)S(1)}, f32[32,32,128]{2,1,0:T(8,128)S(1)}, u32[]{:S(2)}, u32[]{:S(2)}) collective-permute-start(f32[32,32,128]{2,1,0:T(8,128)S(1)} %get-tuple-element.52), channel_id=1, source_target_pairs={{0,4},{4,0},{1,5},{5,1},{2,6},{6,2},{3,7},{7,3},{8,12},{12,8},{9,1... | collective-permute-start | bytes 1572872 | tf_op jit(solution)/shard_map/ppermute | solution.py:36
  32.4 2.2 %shard_map.51 = (f32[4,32,32,128]{3,2,1,0:T(8,128)S(1)}, f32[32,32,128]{2,1,0:T(8,128)S(1)}, f32[4,32,128]{2,1,0:T(8,128)S(1)}, f32[4,64,128]{2,1,0:T(8,128)S(1)}) custom-call(f32[4,64,32,128]{3,2,1,0:T(8,128)S(1)} %get-tuple-element.38.after.refs_0_, f32[4,64,32,128]{3,2,1,0:T(8,128)S(1)} %get-tuple-element.42.refs_1_.refs_2_.north, ...), custom_call_target="tpu_custom_call" | custom-call | flops 10485760 | tf_op jit(solution)/shard_map/pallas_call | solution.py:363
  36.1 2.1 %collective-permute-done.5.refs_5_ = f32[4,32,128]{2,1,0:T(8,128)S(1)} collective-permute-done((f32[4,32,128]{2,1,0:T(8,128)S(1)}, f32[4,32,128]{2,1,0:T(8,128)S(1)}, u32[]{:S(2)}, u32[]{:S(2)}) %collective-permute-start.5) | collective-permute-done | bytes 65568 | tf_op jit(solution)/shard_map/ppermute | solution.py:36
  38.2 6.7 %collective-permute-done.7.refs_7_ = f32[32,32,128]{2,1,0:T(8,128)S(1)} collective-permute-done((f32[32,32,128]{2,1,0:T(8,128)S(1)}, f32[32,32,128]{2,1,0:T(8,128)S(1)}, u32[]{:S(2)}, u32[]{:S(2)}) %collective-permute-start.7) | collective-permute-done | bytes 524320 | tf_op jit(solution)/shard_map/ppermute | solution.py:36
  44.8 2.0 %shard_map.52 = (f32[4,32,32,128]{3,2,1,0:T(8,128)S(1)}, f32[32,32,128]{2,1,0:T(8,128)S(1)}) custom-call(f32[4,32,32,128]{3,2,1,0:T(8,128)S(1)} %get-tuple-element.47.refs_7_.refs_0_, f32[4,32,32,128]{3,2,1,0:T(8,128)S(1)} %get-tuple-element.49.refs_1_, f32[4,64,32,128]{3,2,1,0:T(8,128)S(1)} %get-tuple-element.42.refs_1_.refs_2_.north, ...), custom_call_target="tpu_custom_call" | custom-call | flops 10485760 | tf_op jit(solution)/shard_map/pallas_call | solution.py:363
  46.8 1.5 %collective-permute-start.11 = (f32[32,32,128]{2,1,0:T(8,128)S(1)}, f32[32,32,128]{2,1,0:T(8,128)S(1)}, u32[]{:S(2)}, u32[]{:S(2)}) collective-permute-start(f32[32,32,128]{2,1,0:T(8,128)S(1)} %get-tuple-element.58), channel_id=1, source_target_pairs={{0,4},{4,0},{1,5},{5,1},{2,6},{6,2},{3,7},{7,3},{8,12},{12,8},{9,1... | collective-permute-start | bytes 1572872 | tf_op jit(solution)/shard_map/ppermute | solution.py:36
  48.4 7.7 %collective-permute-done.8.refs_7_ = f32[32,32,128]{2,1,0:T(8,128)S(1)} collective-permute-done((f32[32,32,128]{2,1,0:T(8,128)S(1)}, f32[32,32,128]{2,1,0:T(8,128)S(1)}, u32[]{:S(2)}, u32[]{:S(2)}) %collective-permute-start.8) | collective-permute-done | bytes 524320 | tf_op jit(solution)/shard_map/ppermute | solution.py:36
  56.1 2.2 %shard_map.53 = (f32[4,32,32,128]{3,2,1,0:T(8,128)S(1)}, f32[32,32,128]{2,1,0:T(8,128)S(1)}, f32[4,32,128]{2,1,0:T(8,128)S(1)}, f32[4,64,128]{2,1,0:T(8,128)S(1)}) custom-call(f32[4,32,32,128]{3,2,1,0:T(8,128)S(1)} %get-tuple-element.47.refs_7_.refs_0_, f32[4,32,32,128]{3,2,1,0:T(8,128)S(1)} %get-tuple-element.49.refs_1_, ...), custom_call_target="tpu_custom_call" | custom-call | flops 10485760 | tf_op jit(solution)/shard_map/pallas_call | solution.py:363
  58.2 1.5 %collective-permute-start.12 = (f32[32,32,128]{2,1,0:T(8,128)S(1)}, f32[32,32,128]{2,1,0:T(8,128)S(1)}, u32[]{:S(2)}, u32[]{:S(2)}) collective-permute-start(f32[32,32,128]{2,1,0:T(8,128)S(1)} %get-tuple-element.60), channel_id=1, source_target_pairs={{0,4},{4,0},{1,5},{5,1},{2,6},{6,2},{3,7},{7,3},{8,12},{12,8},{9,1... | collective-permute-start | bytes 1572872 | tf_op jit(solution)/shard_map/ppermute | solution.py:36
  61.0 2.2 %collective-permute-done.9.refs_5_ = f32[4,32,128]{2,1,0:T(8,128)S(1)} collective-permute-done((f32[4,32,128]{2,1,0:T(8,128)S(1)}, f32[4,32,128]{2,1,0:T(8,128)S(1)}, u32[]{:S(2)}, u32[]{:S(2)}) %collective-permute-start.9) | collective-permute-done | bytes 65568 | tf_op jit(solution)/shard_map/ppermute | solution.py:36
  63.2 4.1 %collective-permute-done.11.refs_7_ = f32[32,32,128]{2,1,0:T(8,128)S(1)} collective-permute-done((f32[32,32,128]{2,1,0:T(8,128)S(1)}, f32[32,32,128]{2,1,0:T(8,128)S(1)}, u32[]{:S(2)}, u32[]{:S(2)}) %collective-permute-start.11) | collective-permute-done | bytes 524320 | tf_op jit(solution)/shard_map/ppermute | solution.py:36
  67.3 2.0 %shard_map.54 = (f32[4,32,32,128]{3,2,1,0:T(8,128)S(1)}, f32[32,32,128]{2,1,0:T(8,128)S(1)}) custom-call(f32[4,32,32,128]{3,2,1,0:T(8,128)S(1)} %get-tuple-element.53.refs_8_.refs_0_, f32[4,32,32,128]{3,2,1,0:T(8,128)S(1)} %get-tuple-element.55.refs_1_, f32[4,64,32,128]{3,2,1,0:T(8,128)S(1)} %get-tuple-element.42.refs_1_.refs_2_.north, ...), custom_call_target="tpu_custom_call" | custom-call | flops 10485760 | tf_op jit(solution)/shard_map/pallas_call | solution.py:363
  69.3 1.5 %collective-permute-start.17 = (f32[32,32,128]{2,1,0:T(8,128)S(1)}, f32[32,32,128]{2,1,0:T(8,128)S(1)}, u32[]{:S(2)}, u32[]{:S(2)}) collective-permute-start(f32[32,32,128]{2,1,0:T(8,128)S(1)} %get-tuple-element.67), channel_id=1, source_target_pairs={{0,4},{4,0},{1,5},{5,1},{2,6},{6,2},{3,7},{7,3},{8,12},{12,8},{9,1... | collective-permute-start | bytes 1572872 | tf_op jit(solution)/shard_map/ppermute | solution.py:36
  70.8 7.7 %collective-permute-done.12.refs_7_ = f32[32,32,128]{2,1,0:T(8,128)S(1)} collective-permute-done((f32[32,32,128]{2,1,0:T(8,128)S(1)}, f32[32,32,128]{2,1,0:T(8,128)S(1)}, u32[]{:S(2)}, u32[]{:S(2)}) %collective-permute-start.12) | collective-permute-done | bytes 524320 | tf_op jit(solution)/shard_map/ppermute | solution.py:36
  78.5 2.2 %shard_map.55 = (f32[4,32,32,128]{3,2,1,0:T(8,128)S(1)}, f32[24,32,128]{2,1,0:T(8,128)S(1)}, f32[8,32,128]{2,1,0:T(8,128)S(1)}, f32[4,32,128]{2,1,0:T(8,128)S(1)}, f32[4,64,128]{2,1,0:T(8,128)S(1)}) custom-call(f32[4,32,32,128]{3,2,1,0:T(8,128)S(1)} %get-tuple-element.53.refs_8_.refs_0_, f32[4,32,32,128]{3,2,1,0:T(8,128)S(1)} %get-tuple-element.55.refs_1_, ...), custom_call_target="tpu_custom_call" | custom-call | flops 10485760 | tf_op jit(solution)/shard_map/pallas_call | solution.py:363
  83.7 2.1 %collective-permute-done.13.refs_5_ = f32[4,32,128]{2,1,0:T(8,128)S(1)} collective-permute-done((f32[4,32,128]{2,1,0:T(8,128)S(1)}, f32[4,32,128]{2,1,0:T(8,128)S(1)}, u32[]{:S(2)}, u32[]{:S(2)}) %collective-permute-start.13) | collective-permute-done | bytes 65568 | tf_op jit(solution)/shard_map/ppermute | solution.py:36
  85.8 4.7 %shard_map.56 = (f32[4,64,32,128]{3,2,1,0:T(8,128)}, f32[64,32,128]{2,1,0:T(8,128)S(1)}) custom-call(f32[4,32,32,128]{3,2,1,0:T(8,128)S(1)} %get-tuple-element.59.refs_8_.refs_0_, f32[4,32,32,128]{3,2,1,0:T(8,128)S(1)} %get-tuple-element.61.refs_1_, f32[4,64,32,128]{3,2,1,0:T(8,128)S(1)} %get-tuple-element.42.refs_1_.refs_2_.north, ...), custom_call_target="tpu_custom_call" | custom-call | flops 20971520 | tf_op jit(solution)/shard_map/pallas_call | solution.py:363
  91.4 5.2 %collective-permute-done.16.refs_1_ = f32[24,32,128]{2,1,0:T(8,128)S(1)} collective-permute-done((f32[24,32,128]{2,1,0:T(8,128)S(1)}, f32[24,32,128]{2,1,0:T(8,128)S(1)}, u32[]{:S(2)}, u32[]{:S(2)}) %collective-permute-start.16) | collective-permute-done | bytes 393248 | tf_op jit(solution)/shard_map/ppermute | solution.py:36
  (26 shorter events, 12.6 us)
Async XLA Ops:
  6.8 25.5 %collective-permute-start.4 = (f32[32,32,128]{2,1,0:T(8,128)S(1)}, f32[32,32,128]{2,1,0:T(8,128)S(1)}, u32[]{:S(2)}, u32[]{:S(2)}) collective-permute-start(f32[32,32,128]{2,1,0:T(8,128)S(1)} %get-tuple-element.48), channel_id=1, source_target_pairs={{0,4},{4,0},{1,5},{5,1},{2,6},{6,2},{3,7},{7,3},{8,12},{12,8},{9,1... | collective-permute-start | bytes 1572872 | tf_op jit(solution)/shard_map/ppermute | solution.py:36
  8.9 19.6 %collective-permute-start.3 = (f32[20,32,128]{2,1,0:T(8,128)S(1)}, f32[20,32,128]{2,1,0:T(8,128)S(1)}, u32[]{:S(2)}, u32[]{:S(2)}) collective-permute-start(f32[20,32,128]{2,1,0:T(8,128)S(1)} %get-tuple-element.37.after), channel_id=1, source_target_pairs={{0,4},{4,0},{1,5},{5,1},{2,6},{6,2},{3,7},{7,3},{8,12},{12,8},{9,1... | collective-permute-start | bytes 983048 | tf_op jit(solution)/shard_map/ppermute | solution.py:36
  9.0 19.6 %collective-permute-start.2 = (f32[12,32,128]{2,1,0:T(8,128)S(1)}, f32[12,32,128]{2,1,0:T(8,128)S(1)}, u32[]{:S(2)}, u32[]{:S(2)}) collective-permute-start(f32[12,32,128]{2,1,0:T(8,128)S(1)} %shard_map.46.after), channel_id=1, source_target_pairs={{0,4},{4,0},{1,5},{5,1},{2,6},{6,2},{3,7},{7,3},{8,12},{12,8},{9,1... | collective-permute-start | bytes 589832 | tf_op jit(solution)/shard_map/ppermute | solution.py:36
  12.7 3.6 %collective-permute-start.1 = (f32[4,64,128]{2,1,0:T(8,128)S(1)}, f32[4,64,128]{2,1,0:T(8,128)S(1)}, u32[]{:S(2)}, u32[]{:S(2)}) collective-permute-start(f32[4,64,128]{2,1,0:T(8,128)S(1)} %get-tuple-element.46), channel_id=1, source_target_pairs={{0,1},{1,0},{2,3},{3,2},{4,5},{5,4},{6,7},{7,6},{8,9},{9,8},{10,11... | collective-permute-start | bytes 393224 | tf_op jit(solution)/shard_map/ppermute | solution.py:36
  12.8 3.5 %collective-permute-start = (f32[4,32,128]{2,1,0:T(8,128)S(1)}, f32[4,32,128]{2,1,0:T(8,128)S(1)}, u32[]{:S(2)}, u32[]{:S(2)}) collective-permute-start(f32[4,32,128]{2,1,0:T(8,128)S(1)} %get-tuple-element.45), channel_id=1, source_target_pairs={{0,2},{2,0},{1,3},{3,1},{4,6},{6,4},{5,7},{7,5},{8,10},{10,8},{9,1... | collective-permute-start | bytes 196616 | tf_op jit(solution)/shard_map/ppermute | solution.py:36
  30.6 14.3 %collective-permute-start.7 = (f32[32,32,128]{2,1,0:T(8,128)S(1)}, f32[32,32,128]{2,1,0:T(8,128)S(1)}, u32[]{:S(2)}, u32[]{:S(2)}) collective-permute-start(f32[32,32,128]{2,1,0:T(8,128)S(1)} %get-tuple-element.52), channel_id=1, source_target_pairs={{0,4},{4,0},{1,5},{5,1},{2,6},{6,2},{3,7},{7,3},{8,12},{12,8},{9,1... | collective-permute-start | bytes 1572872 | tf_op jit(solution)/shard_map/ppermute | solution.py:36
  34.5 21.5 %collective-permute-start.8 = (f32[32,32,128]{2,1,0:T(8,128)S(1)}, f32[32,32,128]{2,1,0:T(8,128)S(1)}, u32[]{:S(2)}, u32[]{:S(2)}) collective-permute-start(f32[32,32,128]{2,1,0:T(8,128)S(1)} %get-tuple-element.54), channel_id=1, source_target_pairs={{0,4},{4,0},{1,5},{5,1},{2,6},{6,2},{3,7},{7,3},{8,12},{12,8},{9,1... | collective-permute-start | bytes 1572872 | tf_op jit(solution)/shard_map/ppermute | solution.py:36
  34.6 3.5 %collective-permute-start.6 = (f32[4,64,128]{2,1,0:T(8,128)S(1)}, f32[4,64,128]{2,1,0:T(8,128)S(1)}, u32[]{:S(2)}, u32[]{:S(2)}) collective-permute-start(f32[4,64,128]{2,1,0:T(8,128)S(1)} %get-tuple-element.51), channel_id=1, source_target_pairs={{0,1},{1,0},{2,3},{3,2},{4,5},{5,4},{6,7},{7,6},{8,9},{9,8},{10,11... | collective-permute-start | bytes 393224 | tf_op jit(solution)/shard_map/ppermute | solution.py:36
  34.7 3.5 %collective-permute-start.5 = (f32[4,32,128]{2,1,0:T(8,128)S(1)}, f32[4,32,128]{2,1,0:T(8,128)S(1)}, u32[]{:S(2)}, u32[]{:S(2)}) collective-permute-start(f32[4,32,128]{2,1,0:T(8,128)S(1)} %get-tuple-element.50), channel_id=1, source_target_pairs={{0,2},{2,0},{1,3},{3,1},{4,6},{6,4},{5,7},{7,5},{8,10},{10,8},{9,1... | collective-permute-start | bytes 196616 | tf_op jit(solution)/shard_map/ppermute | solution.py:36
  46.8 20.5 %collective-permute-start.11 = (f32[32,32,128]{2,1,0:T(8,128)S(1)}, f32[32,32,128]{2,1,0:T(8,128)S(1)}, u32[]{:S(2)}, u32[]{:S(2)}) collective-permute-start(f32[32,32,128]{2,1,0:T(8,128)S(1)} %get-tuple-element.58), channel_id=1, source_target_pairs={{0,4},{4,0},{1,5},{5,1},{2,6},{6,2},{3,7},{7,3},{8,12},{12,8},{9,1... | collective-permute-start | bytes 1572872 | tf_op jit(solution)/shard_map/ppermute | solution.py:36
  58.2 20.3 %collective-permute-start.12 = (f32[32,32,128]{2,1,0:T(8,128)S(1)}, f32[32,32,128]{2,1,0:T(8,128)S(1)}, u32[]{:S(2)}, u32[]{:S(2)}) collective-permute-start(f32[32,32,128]{2,1,0:T(8,128)S(1)} %get-tuple-element.60), channel_id=1, source_target_pairs={{0,4},{4,0},{1,5},{5,1},{2,6},{6,2},{3,7},{7,3},{8,12},{12,8},{9,1... | collective-permute-start | bytes 1572872 | tf_op jit(solution)/shard_map/ppermute | solution.py:36
  59.8 3.4 %collective-permute-start.10 = (f32[4,64,128]{2,1,0:T(8,128)S(1)}, f32[4,64,128]{2,1,0:T(8,128)S(1)}, u32[]{:S(2)}, u32[]{:S(2)}) collective-permute-start(f32[4,64,128]{2,1,0:T(8,128)S(1)} %get-tuple-element.57), channel_id=1, source_target_pairs={{0,1},{1,0},{2,3},{3,2},{4,5},{5,4},{6,7},{7,6},{8,9},{9,8},{10,11... | collective-permute-start | bytes 393224 | tf_op jit(solution)/shard_map/ppermute | solution.py:36
  59.8 3.4 %collective-permute-start.9 = (f32[4,32,128]{2,1,0:T(8,128)S(1)}, f32[4,32,128]{2,1,0:T(8,128)S(1)}, u32[]{:S(2)}, u32[]{:S(2)}) collective-permute-start(f32[4,32,128]{2,1,0:T(8,128)S(1)} %get-tuple-element.56), channel_id=1, source_target_pairs={{0,2},{2,0},{1,3},{3,1},{4,6},{6,4},{5,7},{7,5},{8,10},{10,8},{9,1... | collective-permute-start | bytes 196616 | tf_op jit(solution)/shard_map/ppermute | solution.py:36
  69.3 21.2 %collective-permute-start.17 = (f32[32,32,128]{2,1,0:T(8,128)S(1)}, f32[32,32,128]{2,1,0:T(8,128)S(1)}, u32[]{:S(2)}, u32[]{:S(2)}) collective-permute-start(f32[32,32,128]{2,1,0:T(8,128)S(1)} %get-tuple-element.67), channel_id=1, source_target_pairs={{0,4},{4,0},{1,5},{5,1},{2,6},{6,2},{3,7},{7,3},{8,12},{12,8},{9,1... | collective-permute-start | bytes 1572872 | tf_op jit(solution)/shard_map/ppermute | solution.py:36
  80.7 16.0 %collective-permute-start.16 = (f32[24,32,128]{2,1,0:T(8,128)S(1)}, f32[24,32,128]{2,1,0:T(8,128)S(1)}, u32[]{:S(2)}, u32[]{:S(2)}) collective-permute-start(f32[24,32,128]{2,1,0:T(8,128)S(1)} %get-tuple-element.66), channel_id=1, source_target_pairs={{0,4},{4,0},{1,5},{5,1},{2,6},{6,2},{3,7},{7,3},{8,12},{12,8},{9,1... | collective-permute-start | bytes 1179656 | tf_op jit(solution)/shard_map/ppermute | solution.py:36
  82.2 3.6 %collective-permute-start.14 = (f32[4,64,128]{2,1,0:T(8,128)S(1)}, f32[4,64,128]{2,1,0:T(8,128)S(1)}, u32[]{:S(2)}, u32[]{:S(2)}) collective-permute-start(f32[4,64,128]{2,1,0:T(8,128)S(1)} %get-tuple-element.63), channel_id=1, source_target_pairs={{0,1},{1,0},{2,3},{3,2},{4,5},{5,4},{6,7},{7,6},{8,9},{9,8},{10,11... | collective-permute-start | bytes 393224 | tf_op jit(solution)/shard_map/ppermute | solution.py:36
  82.2 15.8 %collective-permute-start.15 = (f32[8,32,128]{2,1,0:T(8,128)S(1)}, f32[8,32,128]{2,1,0:T(8,128)S(1)}, u32[]{:S(2)}, u32[]{:S(2)}) collective-permute-start(f32[8,32,128]{2,1,0:T(8,128)S(1)} %get-tuple-element.65), channel_id=1, source_target_pairs={{0,4},{4,0},{1,5},{5,1},{2,6},{6,2},{3,7},{7,3},{8,12},{12,8},{9,1... | collective-permute-start | bytes 393224 | tf_op jit(solution)/shard_map/ppermute | solution.py:36
  82.4 3.4 %collective-permute-start.13 = (f32[4,32,128]{2,1,0:T(8,128)S(1)}, f32[4,32,128]{2,1,0:T(8,128)S(1)}, u32[]{:S(2)}, u32[]{:S(2)}) collective-permute-start(f32[4,32,128]{2,1,0:T(8,128)S(1)} %get-tuple-element.62), channel_id=1, source_target_pairs={{0,2},{2,0},{1,3},{3,1},{4,6},{6,4},{5,7},{7,5},{8,10},{10,8},{9,1... | collective-permute-start | bytes 196616 | tf_op jit(solution)/shard_map/ppermute | solution.py:36
